TPU v7x, 256 devices: a whole 4x4x8 slice. The times are simulated.
256 devices in a mesh: src: 32 (over y_lo, z, core), tgt: 8 (over x, y_hi).
Axes of the slice: x: 4, y: 4 (y_hi: 2, y_lo: 2; y = y_hi * 2 + y_lo), z: 8, core: 2. Of those that a mesh axis runs over, the one named last changes fastest.
Arguments:
- atom_feats: bfloat16 [2048, 3200], P(('src', 'tgt')), may hold values from -6 to 6
- positions: float32 [3, 2048], P(None, ('src', 'tgt')), may hold values from 0 to 1
- edge_src: int32 [262144], P(('src', 'tgt')), may hold values from 0 to 63
- edge_tgt: int32 [262144], P(('src', 'tgt')), may hold values from 0 to 255
- edge_angle: float32 [262144], P(('src', 'tgt')), may hold values from -3.140625 to 3.140625
- edge_scale: float32 [262144], P(('src', 'tgt')), may hold values from 0.1 to 1
- edge_count: int32 [32, 8], replicated, may hold values from 1 to 1024, as said below
- k_index: int32 [3, 2048], replicated, may hold values from -6 to 6
- k_filter: float32 [2048, 128], replicated, may hold values from -6 to 6
- weight_zero: bfloat16 [2, 640, 640], replicated, may hold values from -0.25 to 0.25
- weight_first: bfloat16 [2, 2, 512, 512], replicated, may hold values from -0.1875 to 0.1875
- weight_second: bfloat16 [2, 2, 384, 384], replicated, may hold values from -0.21875 to 0.21875
- weight_third: bfloat16 [2, 2, 256, 256], replicated, may hold values from -0.25 to 0.25
- weight_fourth: bfloat16 [2, 2, 128, 128], replicated, may hold values from -0.375 to 0.375
Outputs:
- edge_update: bfloat16 [2048, 3200], P(('tgt', 'src'))
- long_range: float32 [2048, 128], P(('src', 'tgt'))
Inputs may be any that keep to these rules, and one draw needn't show every extreme that they name: `edge_count`: live edge slots of tile (s, t); in every draw some tile is full with 1024.
All inputs are finite; a program needn't handle non-finite values.
Results may differ from a plain program's by a relative error of at most 0.0047.
Values may be sent and summed in bfloat16 or wider, within the bound.
No kernel may reach another device: no remote copies, remote signals or barrier semaphores. Data moves between devices by JAX's collectives and lax.ppermute only.
A program may use at most 64 MiB of HBM per device.

v0:
```python
import math

import jax
import jax.numpy as jnp
from jax import lax
from jax.experimental import pallas as pl
from jax.experimental.pallas import tpu as pltpu
from jax.sharding import Mesh
from jax.sharding import PartitionSpec as P

Y, ZH, R, TGT = 2, 4, 4, 8
SRC_AXES = ("y", "zh", "r")
ALL_AXES = ("y", "zh", "r", "tgt")
SRC = Y * ZH * R
SLICES = Y * R
LANES = 128
ROWS = 8
BLOCKS = 25
CH = LANES // SLICES
COLS = BLOCKS * CH
STEP = 256
POS_LANE = 16
COST = {
    "first": pl.CostEstimate(flops=50_000_000, transcendentals=0, bytes_accessed=3_000_000),
    "spread": pl.CostEstimate(flops=0, transcendentals=0, bytes_accessed=800_000),
    "edge_sums": pl.CostEstimate(flops=8_000_000_000, transcendentals=1_500_000, bytes_accessed=2_000_000),
    "last_conv": pl.CostEstimate(flops=100_000_000, transcendentals=0, bytes_accessed=3_200_000),
}
F32 = jnp.float32
BF16 = jnp.bfloat16


def order_spans():
    spans = [(0, 5)]
    offset = 5
    for order in range(1, 5):
        spans.append((offset, 5 - order))
        offset += 2 * (5 - order)
    return spans


SPANS = order_spans()


def sincos_turns(turns):
    part = turns - jnp.floor(turns + 0.5)
    x = part * math.pi
    x2 = x * x
    s = 1.0 / math.factorial(9)
    for k in (7, 5, 3):
        s = s * x2 + (1.0 if k % 4 == 1 else -1.0) / math.factorial(k)
    s = x + x * (x2 * s)
    c = -1.0 / math.factorial(10)
    for k in (8, 6, 4, 2):
        c = c * x2 + (1.0 if k % 4 == 0 else -1.0) / math.factorial(k)
    c = 1.0 + x2 * c
    return 1.0 - 2.0 * s * s, 2.0 * s * c


def split2(value):
    high = value.astype(BF16)
    return high, (value - high.astype(F32)).astype(BF16)


def position_tile(pos_ref):
    row_ids = lax.broadcasted_iota(jnp.int32, (ROWS, ROWS), 0)
    col_ids = lax.broadcasted_iota(jnp.int32, (ROWS, ROWS), 1)
    lane = lax.broadcasted_iota(jnp.int32, (ROWS, LANES), 1)
    tile = jnp.zeros((ROWS, LANES), F32)
    for axis in range(3):
        spread = jnp.broadcast_to(pos_ref[axis : axis + 1, :], (ROWS, ROWS))
        rest = jnp.sum(jnp.where(row_ids == col_ids, spread, 0.0), axis=1, keepdims=True)
        for part in range(3):
            piece = rest.astype(BF16).astype(F32)
            rest = rest - piece
            tile = jnp.where(lane == POS_LANE + 3 * axis + part, piece, tile)
    return tile


def edge_tiles(count_ref, src_ref, tgt_ref, angle_ref, scale_ref):
    group = (lax.axis_index("y") * ZH + lax.axis_index("zh")) * R + lax.axis_index("r")
    count = count_ref[lax.axis_index("tgt"), group]
    slot = lax.broadcasted_iota(jnp.int32, (ROWS, LANES), 0) * LANES + lax.broadcasted_iota(
        jnp.int32, (ROWS, LANES), 1
    )
    angle = angle_ref[...]
    angle_high = angle.astype(BF16).astype(F32)
    return (
        src_ref[...].astype(F32),
        jnp.where(slot < count, tgt_ref[...], SRC * ROWS).astype(F32),
        angle_high,
        angle - angle_high,
        scale_ref[...],
    )


def pair_product(stacked, weight_ref):
    first = jnp.dot(stacked, weight_ref[0], preferred_element_type=F32)
    second = jnp.dot(stacked, weight_ref[1], preferred_element_type=F32)
    lead = jnp.zeros((ROWS, first.shape[1]), F32)
    trail = lead
    for base in range(0, stacked.shape[0], 2 * ROWS):
        lead = lead + (first[base : base + ROWS] - second[base + ROWS : base + 2 * ROWS])
        trail = trail + (second[base : base + ROWS] + first[base + ROWS : base + 2 * ROWS])
    return lead, trail


def first_kernel(count_ref, *refs):
    sources, kfilter_hbm, (out_ref, kslice_ref) = refs[:11], refs[11], refs[12:14]
    held, (conv_ref, sems) = refs[14:25], refs[25:]
    copies = [
        pltpu.make_async_copy(source if index < 6 else source.at[0], to, sems.at[index])
        for index, (source, to) in enumerate(zip(sources, held))
    ]
    for copy in copies:
        copy.start()
    kslice = kslice_ref.shape[0]
    k_start = pl.multiple_of((lax.axis_index("y") * R + lax.axis_index("r")) * kslice, kslice)
    copies.append(pltpu.make_async_copy(kfilter_hbm.at[pl.ds(k_start, kslice), :], kslice_ref, sems.at[11]))
    copies[11].start()
    feats_ref, pos_ref = held[0], held[1]
    for copy in copies[:6]:
        copy.wait()
    pos = position_tile(pos_ref)
    out_ref[:, 4, :, :] = jnp.broadcast_to(feats_ref[:, :LANES][None], (SLICES, ROWS, LANES))
    for index, tile in enumerate(edge_tiles(count_ref, *held[2:6])):
        out_ref[:, 5 + index, :, :] = jnp.broadcast_to(tile.astype(BF16)[None], (SLICES, ROWS, LANES))
    x = feats_ref[...].astype(F32)
    for order in range(5):
        copies[6 + order].wait()
        weight = held[6 + order]
        offset, blocks = SPANS[order]
        start, width = offset * LANES, blocks * LANES
        if order == 0:
            conv_ref[:, :width] = jnp.dot(x[:, :width].astype(BF16), weight[...], preferred_element_type=F32)
            continue
        stacked = jnp.concatenate([x[:, start : start + width], x[:, start + width : start + 2 * width]], axis=0)
        lead, trail = pair_product(stacked.astype(BF16), weight)
        conv_ref[:, start : start + width] = lead
        conv_ref[:, start + width : start + 2 * width] = trail
    place = lax.broadcasted_iota(jnp.int32, (ROWS, LANES), 1) // CH
    for tile_index in range(4):
        for piece in range(SLICES):
            tile = pos if tile_index == 3 else jnp.zeros((ROWS, LANES), F32)
            for within in range(min(8, BLOCKS - 8 * tile_index)):
                block = 8 * tile_index + within
                moved = conv_ref[:, block * LANES : (block + 1) * LANES]
                if within != piece:
                    moved = pltpu.roll(moved, (CH * (within - piece)) % LANES, 1)
                tile = jnp.where(place == within, moved * math.sqrt(0.5), tile)
            out_ref[piece, tile_index, :, :] = tile.astype(BF16)
    copies[11].wait()


def spread_kernel(parts_ref, out_hbm, pos_ref, sems):
    copies = [
        pltpu.make_async_copy(parts_ref.at[:, pl.ds(0, 5)], out_hbm.at[index], sems.at[index]) for index in range(TGT)
    ]
    for copy in copies:
        copy.start()
    pos_ref[...] = parts_ref[:, 3, :, :]
    for copy in copies:
        copy.wait()


def main_kernel(
    count_ref,
    feats_hbm,
    group_ref,
    pos_ref0,
    pos_ref1,
    pos_ref2,
    pos_ref3,
    kidx_ref,
    *refs,
):
    kfilter_ref, out_ref = refs[:2]
    feats_ref, src_ref, tgt_ref, coef_ref, xt_ref, rows_ref, yt_ref, acc_ref, list_ref, sems = refs[2:]
    zone = lax.axis_index("zh")
    piece = lax.axis_index("y") * R + lax.axis_index("r")
    target_group = lax.axis_index("tgt")
    kslice = SRC * ROWS
    k_start = pl.multiple_of(piece * kslice, kslice)
    feats_copy = pltpu.make_async_copy(feats_hbm, feats_ref, sems.at[0])
    feats_copy.start()

    spare = pl.ds(ROWS * SLICES, ROWS)
    src_ref[spare, :] = jnp.zeros((ROWS, LANES), F32)
    tgt_ref[spare, :] = jnp.full((ROWS, LANES), SRC * ROWS, F32)
    for index in range(17):
        coef_ref[index, spare, :] = jnp.zeros((ROWS, LANES), F32)
    for tile in range(SLICES):
        rows = pl.ds(ROWS * tile, ROWS)
        src_ref[rows, :] = group_ref[tile, 5, :, :].astype(F32)
        tgt_ref[rows, :] = group_ref[tile, 6, :, :].astype(F32)
        angle = group_ref[tile, 7, :, :].astype(F32) + group_ref[tile, 8, :, :].astype(F32)
        scale = group_ref[tile, 9, :, :].astype(F32) * math.sqrt(0.5)
        c1, s1 = sincos_turns(angle * (0.5 / math.pi))
        c, s = c1, s1
        coef_ref[16, rows, :] = scale
        for order in range(4):
            if order:
                c, s = c * c1 - s * s1, s * c1 + c * s1
            coef_ref[4 * order, rows, :] = c
            coef_ref[4 * order + 1, rows, :] = s
            coef_ref[4 * order + 2, rows, :] = scale * c
            coef_ref[4 * order + 3, rows, :] = scale * s
    feats_copy.wait()
    for tile in range(SLICES):
        for index in range(4):
            block = feats_ref[:, tile, index, :, :].astype(F32).reshape(TGT * ROWS, LANES)
            width = min(LANES, COLS - index * LANES)
            xt_ref[tile, index * LANES : index * LANES + width, :] = block.T[:width].astype(BF16)

    per_step = STEP // LANES

    def list_tile(tile, at):
        source = (tile // R) * (ZH * R) + zone * R + tile % R
        steps = (count_ref[target_group, source] + STEP - 1) // STEP

        def put(step, place):
            list_ref[place] = tile * ROWS + step * per_step
            return place + 1

        return lax.fori_loop(0, steps, put, at)

    steps = lax.fori_loop(0, SLICES, list_tile, 0)
    list_ref[steps] = ROWS * SLICES

    acc_ref[...] = jnp.zeros_like(acc_ref)
    src_ids = lax.broadcasted_iota(jnp.int32, (TGT * ROWS, STEP), 0).astype(F32)
    tgt_ids = lax.broadcasted_iota(jnp.int32, (SRC * ROWS, 2 * STEP), 0).astype(F32)

    def two_steps(pair, carry):
        starts = [list_ref[2 * pair], list_ref[2 * pair + 1]]
        rows = [start + part for start in starts for part in range(per_step)]

        def lanes_of(rows, ref, *lead):
            return jnp.concatenate([ref[(*lead, pl.ds(row, 1), slice(None))] for row in rows], axis=1)

        for half in range(2):
            lanes = slice(half * STEP, (half + 1) * STEP)
            tile = jnp.minimum(starts[half] // ROWS, SLICES - 1)
            one_src = (src_ids == lanes_of(rows[half * per_step : (half + 1) * per_step], src_ref)).astype(F32)
            rows_ref[:, lanes] = jnp.dot(xt_ref[tile], one_src.astype(BF16), preferred_element_type=F32)
        width = SPANS[0][1] * CH
        scale = lanes_of(rows, coef_ref, 16)
        for low in range(0, width, CH):
            gathered = rows_ref[low : low + CH, :]
            yt_ref[low : low + CH, :] = ((gathered + gathered * lax.erf(gathered)) * scale).astype(BF16)
        for order in range(1, 5):
            offset, blocks = SPANS[order]
            cos_in, sin_in, cos_out, sin_out = (lanes_of(rows, coef_ref, 4 * (order - 1) + part) for part in range(4))
            for block in range(blocks):
                low = (offset + block) * CH
                high = low + blocks * CH
                lead, trail = rows_ref[low : low + CH, :], rows_ref[high : high + CH, :]
                lead, trail = cos_in * lead + sin_in * trail, cos_in * trail - sin_in * lead
                lead, trail = lead + lead * lax.erf(lead), trail + trail * lax.erf(trail)
                yt_ref[low : low + CH, :] = (cos_out * lead - sin_out * trail).astype(BF16)
                yt_ref[high : high + CH, :] = (cos_out * trail + sin_out * lead).astype(BF16)
        one_tgt = (tgt_ids == lanes_of(rows, tgt_ref)).astype(F32).astype(BF16)
        acc_ref[:, :COLS] += lax.dot_general(
            one_tgt, yt_ref[...], (((1,), (1,)), ((), ())), preferred_element_type=F32
        )
        return carry

    lax.fori_loop(0, (steps + 1) // 2, two_steps, 0)
    for index in range(4):
        out_ref[:, index, :, :] = (
            acc_ref[:, index * LANES : (index + 1) * LANES].reshape(SRC, ROWS, LANES).astype(BF16)
        )

    row_ids = lax.broadcasted_iota(jnp.int32, (LANES, kslice), 0)
    k_rows = kidx_ref[:, pl.ds(k_start, kslice)].astype(F32)
    k_table = jnp.zeros((LANES, kslice), F32)
    for axis in range(3):
        start = POS_LANE + 3 * axis
        k_table = jnp.where((row_ids >= start) & (row_ids < start + 3), k_rows[axis : axis + 1, :], k_table)
    atoms = SLICES * TGT * ROWS
    charges = feats_ref[:, :, 4, :, :].reshape(atoms, LANES)
    turns = lax.dot_general(
        k_table.T.astype(BF16),
        feats_ref[:, :, 3, :, :].reshape(atoms, LANES),
        (((1,), (1,)), ((), ())),
        preferred_element_type=F32,
    )
    own_pos = jnp.concatenate(
        [ref[...].reshape(SLICES * ROWS, LANES) for ref in (pos_ref0, pos_ref1, pos_ref2, pos_ref3)], axis=0
    )
    own_turns = jnp.dot(own_pos, k_table.astype(BF16), preferred_element_type=F32)
    total = jnp.zeros((kslice, LANES), F32)
    for table, own_table in zip(sincos_turns(turns), sincos_turns(own_turns)):
        factors = jnp.dot(table.astype(BF16), charges, preferred_element_type=F32)
        own_table = own_table.astype(BF16)
        for part in split2(kfilter_ref[...] * factors):
            total = total + jnp.dot(own_table, part, preferred_element_type=F32)
    for shift in range(ZH):
        from_zone = (zone + ZH - shift) % ZH
        for y in range(Y):
            low = (shift * SLICES + y * R) * ROWS
            out_ref[pl.ds(y * ZH * R + from_zone * R, R), 4, :, :] = (
                total[low : low + R * ROWS].reshape(R, ROWS, LANES).astype(BF16)
            )


def last_conv_kernel(norm, parts_ref, w0, w1, w2, w3, w4, update_ref, long_ref, conv_ref):
    total = jnp.zeros((ROWS, LANES), F32)
    for source in range(SRC):
        total = total + parts_ref[source, 4, :, :].astype(F32)
    long_ref[...] = total * norm
    place = lax.broadcasted_iota(jnp.int32, (ROWS, LANES), 1) // CH
    for index in range(4):
        sums = []
        for piece in range(SLICES):
            total = jnp.zeros((ROWS, LANES), F32)
            for zone in range(ZH):
                source = (piece // R) * (ZH * R) + zone * R + piece % R
                total = total + parts_ref[source, index, :, :].astype(F32)
            sums.append(total)
        for within in range(min(8, BLOCKS - 8 * index)):
            block = 8 * index + within
            tile = jnp.zeros((ROWS, LANES), F32)
            for piece in range(SLICES):
                moved = sums[piece]
                if within != piece:
                    moved = pltpu.roll(moved, (CH * (piece - within)) % LANES, 1)
                tile = jnp.where(place == piece, moved, tile)
            conv_ref[:, block * LANES : (block + 1) * LANES] = tile
    width = SPANS[0][1] * LANES
    value = conv_ref[:, :width]
    rounded = value.astype(BF16).astype(F32)
    stacked = jnp.concatenate([rounded, value - rounded], axis=0).astype(BF16)
    product = jnp.dot(stacked, w0[1], preferred_element_type=F32)
    update_ref[:, :width] = (product[:ROWS] + product[ROWS:]).astype(BF16)
    for order, weight in zip(range(1, 5), (w1, w2, w3, w4)):
        offset, blocks = SPANS[order]
        start, width = offset * LANES, blocks * LANES
        lead, trail = conv_ref[:, start : start + width], conv_ref[:, start + width : start + 2 * width]
        lead_high, trail_high = lead.astype(BF16).astype(F32), trail.astype(BF16).astype(F32)
        stacked = jnp.concatenate([lead_high, trail_high, lead - lead_high, trail - trail_high], axis=0)
        lead, trail = pair_product(stacked.astype(BF16), weight.at[1])
        update_ref[:, start : start + width] = lead.astype(BF16)
        update_ref[:, start + width : start + 2 * width] = trail.astype(BF16)


def params(mib):
    return pltpu.CompilerParams(vmem_limit_bytes=mib << 20)


def body(
    atom_feats,
    positions,
    edge_src,
    edge_tgt,
    edge_angle,
    edge_scale,
    edge_count,
    k_index,
    k_filter,
    *weights,
):
    slots = edge_src.shape[0]
    columns = atom_feats.shape[1]
    tile_shape = (ROWS, slots // ROWS)
    smem = pl.BlockSpec(memory_space=pltpu.SMEM)
    vmem = pl.BlockSpec(memory_space=pltpu.VMEM)
    hbm = pl.BlockSpec(memory_space=pltpu.HBM)
    counts = edge_count.T
    group_out = (SLICES, 10, ROWS, LANES)
    sources = (atom_feats, positions) + tuple(
        value.reshape(tile_shape) for value in (edge_src, edge_tgt, edge_angle, edge_scale)
    )
    kslice = SRC * ROWS
    group, k_filter = pl.pallas_call(
        first_kernel,
        out_shape=(jax.ShapeDtypeStruct(group_out, BF16), jax.ShapeDtypeStruct((kslice, LANES), F32)),
        in_specs=[smem] + [hbm] * 12,
        out_specs=(vmem, vmem),
        scratch_shapes=[pltpu.VMEM(value.shape, value.dtype) for value in sources]
        + [pltpu.VMEM(weight.shape[1:], weight.dtype) for weight in weights]
        + [pltpu.VMEM((ROWS, columns), F32), pltpu.SemaphoreType.DMA((12,))],
        compiler_params=params(56),
        cost_estimate=COST["first"],
        name="first",
    )(counts, *sources, *weights, k_filter)
    group = lax.all_to_all(group, ("y", "r"), 0, 0)
    feats_out = (TGT, SLICES, 5, ROWS, LANES)
    pos_out = (SLICES, ROWS, LANES)
    feats, pos = pl.pallas_call(
        spread_kernel,
        out_shape=(jax.ShapeDtypeStruct(feats_out, BF16), jax.ShapeDtypeStruct(pos_out, BF16)),
        in_specs=[vmem],
        out_specs=(hbm, vmem),
        scratch_shapes=[pltpu.SemaphoreType.DMA((TGT,))],
        compiler_params=params(32),
        cost_estimate=COST["spread"],
        name="spread",
    )(group)
    feats = lax.all_to_all(feats, "tgt", 0, 0)
    zones = [pos]
    for shift in range(1, ZH):
        zones.append(lax.ppermute(pos, "zh", [(i, (i + shift) % ZH) for i in range(ZH)]))

    parts_out = (SRC, 5, ROWS, LANES)
    parts = pl.pallas_call(
        main_kernel,
        out_shape=jax.ShapeDtypeStruct(parts_out, BF16),
        in_specs=[smem, hbm] + [vmem] * 7,
        out_specs=vmem,
        scratch_shapes=[
            pltpu.VMEM(feats_out, BF16),
            pltpu.VMEM(((SLICES + 1) * ROWS, LANES), F32),
            pltpu.VMEM(((SLICES + 1) * ROWS, LANES), F32),
            pltpu.VMEM((17, (SLICES + 1) * ROWS, LANES), F32),
            pltpu.VMEM((SLICES, COLS, TGT * ROWS), BF16),
            pltpu.VMEM((COLS, 2 * STEP), F32),
            pltpu.VMEM((COLS, 2 * STEP), BF16),
            pltpu.VMEM((kslice, 4 * LANES), F32),
            pltpu.SMEM((SLICES * (slots // STEP) + 1,), jnp.int32),
            pltpu.SemaphoreType.DMA((1,)),
        ],
        compiler_params=params(32),
        cost_estimate=COST["edge_sums"],
        name="edge_sums",
    )(counts, feats, group, *zones, k_index, k_filter)
    parts = lax.all_to_all(parts, SRC_AXES, 0, 0)

    norm = 1.0 / math.sqrt(SRC * TGT * ROWS * k_index.shape[1])
    return pl.pallas_call(
        lambda *refs: last_conv_kernel(norm, *refs),
        out_shape=(
            jax.ShapeDtypeStruct((ROWS, columns), BF16),
            jax.ShapeDtypeStruct((ROWS, LANES), F32),
        ),
        in_specs=[vmem] * 6,
        out_specs=(vmem, vmem),
        scratch_shapes=[pltpu.VMEM((ROWS, columns), F32)],
        compiler_params=params(16),
        cost_estimate=COST["last_conv"],
        name="last_conv",
    )(parts, *weights)


def solution(mesh):
    fine = Mesh(mesh.devices.reshape(Y, ZH, R, TGT), ALL_AXES)
    return jax.shard_map(
        body,
        mesh=fine,
        in_specs=(P(ALL_AXES, None), P(None, ALL_AXES)) + (P(ALL_AXES),) * 4 + (P(),) * 8,
        out_specs=(P(("tgt",) + SRC_AXES, None), P(ALL_AXES, None)),
        check_vma=False,
    )
```

profile of v0, /device:TPU:1, one launch (start us, length us, event | category | flops | bytes accessed | tf_op | source)
XLA Modules:
  0.0 65.7 jit_solution(5751393484733276738)
XLA Ops:
  0.6 4.0 %first.1 = (bf16[8,10,8,128]{3,2,1,0:T(8,128)(2,1)}, f32[256,128]{1,0:T(8,128)}) custom-call(s32[8,32]{1,0:T(8,128)} %bitcast.5, bf16[8,3200]{1,0:T(8,128)(2,1)} %refs_0_.1, f32[3,8]{1,0:T(4,128)} %refs_1_.2, s32[8,128]{1,0:T(8,128)} %bitcast.7, s32[8,128]{1,0:T(8,128)} %bitcast.8, f32[8,128]{1,0:T(8,128)} %bitcast.9, f32[8,128]{1,0:T(8,128)} %bitcast.10, ...), custom_call_target="tpu_custom_call" | custom-call | flops 50000000 | bytes 3000000 | tf_op jit(solution)/shard_map/first/pallas_call | solution.py:375
  4.6 0.0 copy-start.5
  4.6 0.0 copy-start.6
  4.6 0.0 copy-start.7
  4.7 11.5 %all_to_all.15.parts_ref.group_ref = bf16[8,10,8,128]{3,2,1,0:T(8,128)(2,1)S(1)} all-to-all(bf16[8,10,8,128]{3,2,1,0:T(8,128)(2,1)} %get-tuple-element.6), channel_id=1, replica_groups=mesh['y'=2,'zh'=4,'r'=4,'tgt'=8] {'y','r'}, dimensions={0} | all-to-all | bytes 327680 | tf_op jit(solution)/shard_map/all_to_all | solution.py:387
  16.2 0.9 %spread.1 = (bf16[8,8,5,8,128]{4,3,2,1,0:T(8,128)(2,1)}, bf16[8,8,128]{2,1,0:T(8,128)(2,1)S(1)}) custom-call(bf16[8,10,8,128]{3,2,1,0:T(8,128)(2,1)S(1)} %all_to_all.15.parts_ref.group_ref), custom_call_target="tpu_custom_call" | custom-call | bytes 800000 | tf_op jit(solution)/shard_map/spread/pallas_call | solution.py:390
  17.1 5.6 %all-to-all-start.1 = ((bf16[8,8,5,8,128]{4,3,2,1,0:T(8,128)(2,1)}), bf16[8,8,5,8,128]{4,3,2,1,0:T(8,128)(2,1)S(1)}, u32[]{:S(2)}, u32[]{:S(2)}) async-start(bf16[8,8,5,8,128]{4,3,2,1,0:T(8,128)(2,1)} %get-tuple-element.7), calls=%async_computation.1 | async-start | bytes 1310720 | tf_op jit(solution)/shard_map/all_to_all | solution.py:400
  22.7 5.4 %collective-permute-start.2 = (bf16[8,8,128]{2,1,0:T(8,128)(2,1)S(1)}, bf16[8,8,128]{2,1,0:T(8,128)(2,1)S(1)}, u32[]{:S(2)}, u32[]{:S(2)}) collective-permute-start(bf16[8,8,128]{2,1,0:T(8,128)(2,1)S(1)} %get-tuple-element.8.pos_ref0), channel_id=1, source_target_pairs={{0,96},{32,0},{64,32},{96,64},{1,97},{33,1},{65,33},{97,65},{2,98}... | collective-permute-start | bytes 49160 | tf_op jit(solution)/shard_map/ppermute | solution.py:403
  28.1 1.0 %collective-permute-start.1 = (bf16[8,8,128]{2,1,0:T(8,128)(2,1)S(1)}, bf16[8,8,128]{2,1,0:T(8,128)(2,1)S(1)}, u32[]{:S(2)}, u32[]{:S(2)}) collective-permute-start(bf16[8,8,128]{2,1,0:T(8,128)(2,1)S(1)} %get-tuple-element.8.pos_ref0), channel_id=1, source_target_pairs={{0,64},{32,96},{64,0},{96,32},{1,65},{33,97},{65,1},{97,33},{2,66}... | collective-permute-start | bytes 49160 | tf_op jit(solution)/shard_map/ppermute | solution.py:403
  29.1 2.3 %collective-permute-start = (bf16[8,8,128]{2,1,0:T(8,128)(2,1)S(1)}, bf16[8,8,128]{2,1,0:T(8,128)(2,1)S(1)}, u32[]{:S(2)}, u32[]{:S(2)}) collective-permute-start(bf16[8,8,128]{2,1,0:T(8,128)(2,1)S(1)} %get-tuple-element.8.pos_ref0), channel_id=1, source_target_pairs={{0,32},{32,64},{64,96},{96,0},{1,33},{33,65},{65,97},{97,1},{2,34}... | collective-permute-start | bytes 49160 | tf_op jit(solution)/shard_map/ppermute | solution.py:403
  31.3 0.0 collective-permute-done.2.pos_ref3
  31.3 3.5 %collective-permute-done.1.pos_ref2 = bf16[8,8,128]{2,1,0:T(8,128)(2,1)S(1)} collective-permute-done((bf16[8,8,128]{2,1,0:T(8,128)(2,1)S(1)}, bf16[8,8,128]{2,1,0:T(8,128)(2,1)S(1)}, u32[]{:S(2)}, u32[]{:S(2)}) %collective-permute-start.1) | collective-permute-done | bytes 16416 | tf_op jit(solution)/shard_map/ppermute | solution.py:403
  34.9 0.0 collective-permute-done.pos_ref1
  34.9 0.0 all-to-all-done.1.feats_hbm
  34.9 0.0 copy-done.5
  34.9 0.0 copy-done.6
  34.9 0.0 copy-done.7
  34.9 0.0 copy-start
  34.9 0.0 copy-start.1
  34.9 0.0 copy-start.2
  34.9 0.0 copy-start.3
  34.9 0.0 copy-start.4
  35.0 6.6 %edge_sums.1 = bf16[32,5,8,128]{3,2,1,0:T(8,128)(2,1)S(1)} custom-call(s32[8,32]{1,0:T(8,128)S(1)} %bitcast.6, bf16[8,8,5,8,128]{4,3,2,1,0:T(8,128)(2,1)S(1)} %all-to-all-done.1.feats_hbm, bf16[8,10,8,128]{3,2,1,0:T(8,128)(2,1)S(1)} %all_to_all.15.parts_ref.group_ref, bf16[8,8,128]{2,1,0:T(8,128)(2,1)S(1)} %get-tuple-element.8.pos_ref0, ...), custom_call_target="tpu_custom_call" | custom-call | flops 8000000000 | bytes 2000000 | tf_op jit(solution)/shard_map/edge_sums/pallas_call | solution.py:406
  41.5 22.9 %all_to_all.16.refs_0_ = bf16[32,5,8,128]{3,2,1,0:T(8,128)(2,1)S(1)} all-to-all(bf16[32,5,8,128]{3,2,1,0:T(8,128)(2,1)S(1)} %edge_sums.1), channel_id=1, replica_groups=mesh['y'=2,'zh'=4,'r'=4,'tgt'=8] {'y','zh','r'}, dimensions={0} | all-to-all | bytes 655360 | tf_op jit(solution)/shard_map/all_to_all | solution.py:427
  64.5 0.0 copy-done
  64.5 0.0 copy-done.1
  64.5 0.0 copy-done.2
  64.5 0.0 copy-done.3
  64.5 0.0 copy-done.4
  64.5 1.2 %last_conv.1 = (bf16[8,3200]{1,0:T(8,128)(2,1)}, f32[8,128]{1,0:T(8,128)}) custom-call(bf16[32,5,8,128]{3,2,1,0:T(8,128)(2,1)S(1)} %all_to_all.16.refs_0_, bf16[2,640,640]{2,1,0:T(8,128)(2,1)S(1)} %copy-done.1, bf16[2,2,512,512]{3,2,1,0:T(8,128)(2,1)S(1)} %copy-done, bf16[2,2,384,384]{3,2,1,0:T(8,128)(2,1)S(1)} %copy-done.2, ...), custom_call_target="tpu_custom_call" | custom-call | flops 100000000 | bytes 3200000 | tf_op jit(solution)/shard_map/last_conv/pallas_call | solution.py:430
Async XLA Ops:
  4.6 30.3 %copy-start.5 = (s32[32,8]{0,1:T(8,128)S(1)}, s32[32,8]{0,1:T(8,128)}, u32[]{:S(2)}) copy-start(s32[32,8]{0,1:T(8,128)} %param.20) | copy-start | bytes 3076
  4.6 30.2 %copy-start.6 = (f32[256,128]{1,0:T(8,128)S(1)}, f32[256,128]{1,0:T(8,128)}, u32[]{:S(2)}) copy-start(f32[256,128]{1,0:T(8,128)} %get-tuple-element.9.refs_0_) | copy-start | bytes 393220
  4.6 30.2 %copy-start.7 = (s32[3,2048]{1,0:T(4,128)S(1)}, s32[3,2048]{1,0:T(4,128)}, u32[]{:S(2)}) copy-start(s32[3,2048]{1,0:T(4,128)} %kidx_ref.1) | copy-start | bytes 73732
  17.1 17.8 %all-to-all-start.1 = ((bf16[8,8,5,8,128]{4,3,2,1,0:T(8,128)(2,1)}), bf16[8,8,5,8,128]{4,3,2,1,0:T(8,128)(2,1)S(1)}, u32[]{:S(2)}, u32[]{:S(2)}) async-start(bf16[8,8,5,8,128]{4,3,2,1,0:T(8,128)(2,1)} %get-tuple-element.7), calls=%async_computation.1 | async-start | bytes 1310720 | tf_op jit(solution)/shard_map/all_to_all | solution.py:400
  22.7 8.7 %collective-permute-start.2 = (bf16[8,8,128]{2,1,0:T(8,128)(2,1)S(1)}, bf16[8,8,128]{2,1,0:T(8,128)(2,1)S(1)}, u32[]{:S(2)}, u32[]{:S(2)}) collective-permute-start(bf16[8,8,128]{2,1,0:T(8,128)(2,1)S(1)} %get-tuple-element.8.pos_ref0), channel_id=1, source_target_pairs={{0,96},{32,0},{64,32},{96,64},{1,97},{33,1},{65,33},{97,65},{2,98}... | collective-permute-start | bytes 49160 | tf_op jit(solution)/shard_map/ppermute | solution.py:403
  28.1 6.8 %collective-permute-start.1 = (bf16[8,8,128]{2,1,0:T(8,128)(2,1)S(1)}, bf16[8,8,128]{2,1,0:T(8,128)(2,1)S(1)}, u32[]{:S(2)}, u32[]{:S(2)}) collective-permute-start(bf16[8,8,128]{2,1,0:T(8,128)(2,1)S(1)} %get-tuple-element.8.pos_ref0), channel_id=1, source_target_pairs={{0,64},{32,96},{64,0},{96,32},{1,65},{33,97},{65,1},{97,33},{2,66}... | collective-permute-start | bytes 49160 | tf_op jit(solution)/shard_map/ppermute | solution.py:403
  29.1 5.8 %collective-permute-start = (bf16[8,8,128]{2,1,0:T(8,128)(2,1)S(1)}, bf16[8,8,128]{2,1,0:T(8,128)(2,1)S(1)}, u32[]{:S(2)}, u32[]{:S(2)}) collective-permute-start(bf16[8,8,128]{2,1,0:T(8,128)(2,1)S(1)} %get-tuple-element.8.pos_ref0), channel_id=1, source_target_pairs={{0,32},{32,64},{64,96},{96,0},{1,33},{33,65},{65,97},{97,1},{2,34}... | collective-permute-start | bytes 49160 | tf_op jit(solution)/shard_map/ppermute | solution.py:403
  34.9 29.6 %copy-start = (bf16[2,2,512,512]{3,2,1,0:T(8,128)(2,1)S(1)}, bf16[2,2,512,512]{3,2,1,0:T(8,128)(2,1)}, u32[]{:S(2)}) copy-start(bf16[2,2,512,512]{3,2,1,0:T(8,128)(2,1)} %refs_2_.1) | copy-start | bytes 6291460
  34.9 29.6 %copy-start.1 = (bf16[2,640,640]{2,1,0:T(8,128)(2,1)S(1)}, bf16[2,640,640]{2,1,0:T(8,128)(2,1)}, u32[]{:S(2)}) copy-start(bf16[2,640,640]{2,1,0:T(8,128)(2,1)} %refs_1_.3) | copy-start | bytes 4915204
  34.9 29.5 %copy-start.2 = (bf16[2,2,384,384]{3,2,1,0:T(8,128)(2,1)S(1)}, bf16[2,2,384,384]{3,2,1,0:T(8,128)(2,1)}, u32[]{:S(2)}) copy-start(bf16[2,2,384,384]{3,2,1,0:T(8,128)(2,1)} %refs_3_.1) | copy-start | bytes 3538948
  34.9 29.5 %copy-start.3 = (bf16[2,2,256,256]{3,2,1,0:T(8,128)(2,1)S(1)}, bf16[2,2,256,256]{3,2,1,0:T(8,128)(2,1)}, u32[]{:S(2)}) copy-start(bf16[2,2,256,256]{3,2,1,0:T(8,128)(2,1)} %refs_4_.1) | copy-start | bytes 1572868
  34.9 29.5 %copy-start.4 = (bf16[2,2,128,128]{3,2,1,0:T(8,128)(2,1)S(1)}, bf16[2,2,128,128]{3,2,1,0:T(8,128)(2,1)}, u32[]{:S(2)}) copy-start(bf16[2,2,128,128]{3,2,1,0:T(8,128)(2,1)} %refs_5_.1) | copy-start | bytes 393220
where the time goes:
time: 66.1 us; the launch traced here: 65.7 us
  blocking collectives  34.4 us (52%)
  starting transfers between devices  14.2 us (21%)
  Pallas kernels  12.7 us (19%)
  waiting for transfers between devices  3.54 us (5%)
  between operations  0.76 us (1%)
    all_to_all x1, blocking collectives, body(): parts = lax.all_to_all(parts, SRC_AXES, 0, 0)  22.9 us
    all_to_all x1, blocking collectives, body(): group = lax.all_to_all(group, ('y', 'r'), 0, 0)  11.5 us
    ppermute x3, starting transfers between devices, body(): lax.ppermute(pos, 'zh', [(i, (i + shift) % ZH) for i in range(ZH)])  8.66 us
    pallas_call x1, Pallas kernels, body(): pl.pallas_call(main_kernel, out_shape=jax.ShapeDtypeStruct(parts_out, BF1...  6.57 us
    all_to_all x1, starting transfers between devices, body(): feats = lax.all_to_all(feats, 'tgt', 0, 0)  5.57 us
    pallas_call x1, Pallas kernels, body(): pl.pallas_call(first_kernel, out_shape=(jax.ShapeDtypeStruct(group_out, B...  3.98 us
    ppermute x3, waiting for transfers between devices, body(): lax.ppermute(pos, 'zh', [(i, (i + shift) % ZH) for i in range(ZH)])  3.54 us
  transfers between devices with their start and end apart: 4, of which 1 were waited for; matrix products, arithmetic and copies ran while one was open for 0% of the time, Pallas kernels for 0%

commit v1 on v0

--- a/solution.py
+++ b/solution.py
@@ -18,12 +18,16 @@
 BLOCKS = 25
 CH = LANES // SLICES
 COLS = BLOCKS * CH
+HALF = 208
+CUT = 256
 STEP = 256
 POS_LANE = 16
+LAST_TILE, POS_TILE, CHARGE_TILE, TILES = 24, 25, 26, 34
 COST = {
     "first": pl.CostEstimate(flops=50_000_000, transcendentals=0, bytes_accessed=3_000_000),
     "spread": pl.CostEstimate(flops=0, transcendentals=0, bytes_accessed=800_000),
     "edge_sums": pl.CostEstimate(flops=8_000_000_000, transcendentals=1_500_000, bytes_accessed=2_000_000),
+    "message": pl.CostEstimate(flops=3_000_000_000, transcendentals=400_000, bytes_accessed=1_000_000),
     "last_conv": pl.CostEstimate(flops=100_000_000, transcendentals=0, bytes_accessed=3_200_000),
 }
 F32 = jnp.float32
@@ -42,19 +46,22 @@
 SPANS = order_spans()
 
 
+SIN_TERMS = (4.442867903, -7.307443419, 3.59478806, -0.7843739803)
+COS_TERMS = (1.414213497, -6.978850988, 5.739461171, -1.88356299, 0.3106981923)
+
+
+def series(terms, x2):
+    value = terms[-1]
+    for term in terms[-2::-1]:
+        value = value * x2 + term
+    return value
+
+
 def sincos_turns(turns):
     part = turns - jnp.floor(turns + 0.5)
-    x = part * math.pi
-    x2 = x * x
-    s = 1.0 / math.factorial(9)
-    for k in (7, 5, 3):
-        s = s * x2 + (1.0 if k % 4 == 1 else -1.0) / math.factorial(k)
-    s = x + x * (x2 * s)
-    c = -1.0 / math.factorial(10)
-    for k in (8, 6, 4, 2):
-        c = c * x2 + (1.0 if k % 4 == 0 else -1.0) / math.factorial(k)
-    c = 1.0 + x2 * c
-    return 1.0 - 2.0 * s * s, 2.0 * s * c
+    x2 = part * part
+    s = part * series(SIN_TERMS, x2)
+    return 1.0 - s * s, s * series(COS_TERMS, x2)
 
 
 def split2(value):
@@ -126,20 +133,9 @@
     for index, tile in enumerate(edge_tiles(count_ref, *held[2:6])):
         out_ref[:, 5 + index, :, :] = jnp.broadcast_to(tile.astype(BF16)[None], (SLICES, ROWS, LANES))
     x = feats_ref[...].astype(F32)
-    for order in range(5):
-        copies[6 + order].wait()
-        weight = held[6 + order]
-        offset, blocks = SPANS[order]
-        start, width = offset * LANES, blocks * LANES
-        if order == 0:
-            conv_ref[:, :width] = jnp.dot(x[:, :width].astype(BF16), weight[...], preferred_element_type=F32)
-            continue
-        stacked = jnp.concatenate([x[:, start : start + width], x[:, start + width : start + 2 * width]], axis=0)
-        lead, trail = pair_product(stacked.astype(BF16), weight)
-        conv_ref[:, start : start + width] = lead
-        conv_ref[:, start + width : start + 2 * width] = trail
     place = lax.broadcasted_iota(jnp.int32, (ROWS, LANES), 1) // CH
-    for tile_index in range(4):
+
+    def emit(tile_index):
         for piece in range(SLICES):
             tile = pos if tile_index == 3 else jnp.zeros((ROWS, LANES), F32)
             for within in range(min(8, BLOCKS - 8 * tile_index)):
@@ -147,18 +143,48 @@
                 moved = conv_ref[:, block * LANES : (block + 1) * LANES]
                 if within != piece:
                     moved = pltpu.roll(moved, (CH * (within - piece)) % LANES, 1)
-                tile = jnp.where(place == within, moved * math.sqrt(0.5), tile)
+                tile = jnp.where(place == within, moved, tile)
             out_ref[piece, tile_index, :, :] = tile.astype(BF16)
+
+    root = math.sqrt(0.5)
+    for order in range(5):
+        copies[6 + order].wait()
+        weight = held[6 + order]
+        offset, blocks = SPANS[order]
+        start, width = offset * LANES, blocks * LANES
+        if order == 0:
+            conv_ref[:, :width] = root * jnp.dot(x[:, :width].astype(BF16), weight[...], preferred_element_type=F32)
+            continue
+        stacked = jnp.concatenate([x[:, start : start + width], x[:, start + width : start + 2 * width]], axis=0)
+        lead, trail = pair_product(stacked.astype(BF16), weight)
+        conv_ref[:, start : start + width] = root * lead
+        conv_ref[:, start + width : start + 2 * width] = root * trail
+    for tile_index in range(4):
+        emit(tile_index)
     copies[11].wait()
 
 
-def spread_kernel(parts_ref, out_hbm, pos_ref, sems):
-    copies = [
-        pltpu.make_async_copy(parts_ref.at[:, pl.ds(0, 5)], out_hbm.at[index], sems.at[index]) for index in range(TGT)
-    ]
+def group_lanes(tiles, first_lane):
+    place = lax.broadcasted_iota(jnp.int32, (ROWS, LANES), 1) // CH
+    packed = jnp.zeros((ROWS, LANES), F32)
+    for index, tile in enumerate(tiles):
+        shift = (CH * index - first_lane) % LANES
+        packed = jnp.where(place == index, pltpu.roll(tile, shift, 1) if shift else tile, packed)
+    return packed.astype(BF16)
+
+
+def spread_kernel(parts_ref, out_hbm, pos_ref, held_ref, sems):
+    mixed = [parts_ref[source, 3, :, :].astype(F32) for source in range(SLICES)]
+    pos = group_lanes(mixed, POS_LANE)
+    pos_ref[...] = pos
+    for source in range(SLICES):
+        held_ref[3 * source : 3 * source + 3, :, :] = parts_ref[source, :3, :, :]
+        held_ref[CHARGE_TILE + source, :, :] = parts_ref[source, 4, :, :]
+    held_ref[LAST_TILE, :, :] = group_lanes(mixed, 0)
+    held_ref[POS_TILE, :, :] = pos
+    copies = [pltpu.make_async_copy(held_ref, out_hbm.at[index], sems.at[index]) for index in range(TGT)]
     for copy in copies:
         copy.start()
-    pos_ref[...] = parts_ref[:, 3, :, :]
     for copy in copies:
         copy.wait()
 
@@ -167,20 +193,20 @@
     count_ref,
     feats_hbm,
     group_ref,
-    pos_ref0,
-    pos_ref1,
-    pos_ref2,
-    pos_ref3,
-    kidx_ref,
-    *refs,
+    out_ref,
+    feats_ref,
+    src_ref,
+    tgt_ref,
+    coef_ref,
+    xt_ref,
+    rows_ref,
+    yt_ref,
+    acc_ref,
+    list_ref,
+    sems,
 ):
-    kfilter_ref, out_ref = refs[:2]
-    feats_ref, src_ref, tgt_ref, coef_ref, xt_ref, rows_ref, yt_ref, acc_ref, list_ref, sems = refs[2:]
     zone = lax.axis_index("zh")
-    piece = lax.axis_index("y") * R + lax.axis_index("r")
     target_group = lax.axis_index("tgt")
-    kslice = SRC * ROWS
-    k_start = pl.multiple_of(piece * kslice, kslice)
     feats_copy = pltpu.make_async_copy(feats_hbm, feats_ref, sems.at[0])
     feats_copy.start()
 
@@ -206,11 +232,12 @@
             coef_ref[4 * order + 2, rows, :] = scale * c
             coef_ref[4 * order + 3, rows, :] = scale * s
     feats_copy.wait()
+    last = feats_ref[:, LAST_TILE, :, :].reshape(TGT * ROWS, LANES).T
     for tile in range(SLICES):
-        for index in range(4):
-            block = feats_ref[:, tile, index, :, :].astype(F32).reshape(TGT * ROWS, LANES)
-            width = min(LANES, COLS - index * LANES)
-            xt_ref[tile, index * LANES : index * LANES + width, :] = block.T[:width].astype(BF16)
+        for index in range(3):
+            block = feats_ref[:, 3 * tile + index, :, :].reshape(TGT * ROWS, LANES)
+            xt_ref[tile, index * LANES : (index + 1) * LANES, :] = block.T
+        xt_ref[tile, 3 * LANES :, :] = last[tile * CH : (tile + 1) * CH]
 
     per_step = STEP // LANES
 
@@ -224,69 +251,112 @@
 
         return lax.fori_loop(0, steps, put, at)
 
-    steps = lax.fori_loop(0, SLICES, list_tile, 0)
-    list_ref[steps] = ROWS * SLICES
+    for place in range(2):
+        list_ref[place] = ROWS * SLICES
+    end = lax.fori_loop(0, SLICES, list_tile, 2)
+    for extra in range(3):
+        list_ref[end + extra] = ROWS * SLICES
+    pairs = (end - 1) // 2
 
     acc_ref[...] = jnp.zeros_like(acc_ref)
+    yt_ref[...] = jnp.zeros_like(yt_ref)
     src_ids = lax.broadcasted_iota(jnp.int32, (TGT * ROWS, STEP), 0).astype(F32)
     tgt_ids = lax.broadcasted_iota(jnp.int32, (SRC * ROWS, 2 * STEP), 0).astype(F32)
 
-    def two_steps(pair, carry):
-        starts = [list_ref[2 * pair], list_ref[2 * pair + 1]]
-        rows = [start + part for start in starts for part in range(per_step)]
-
-        def lanes_of(rows, ref, *lead):
-            return jnp.concatenate([ref[(*lead, pl.ds(row, 1), slice(None))] for row in rows], axis=1)
-
-        for half in range(2):
-            lanes = slice(half * STEP, (half + 1) * STEP)
-            tile = jnp.minimum(starts[half] // ROWS, SLICES - 1)
-            one_src = (src_ids == lanes_of(rows[half * per_step : (half + 1) * per_step], src_ref)).astype(F32)
-            rows_ref[:, lanes] = jnp.dot(xt_ref[tile], one_src.astype(BF16), preferred_element_type=F32)
-        width = SPANS[0][1] * CH
-        scale = lanes_of(rows, coef_ref, 16)
-        for low in range(0, width, CH):
-            gathered = rows_ref[low : low + CH, :]
-            yt_ref[low : low + CH, :] = ((gathered + gathered * lax.erf(gathered)) * scale).astype(BF16)
-        for order in range(1, 5):
-            offset, blocks = SPANS[order]
-            cos_in, sin_in, cos_out, sin_out = (lanes_of(rows, coef_ref, 4 * (order - 1) + part) for part in range(4))
-            for block in range(blocks):
-                low = (offset + block) * CH
-                high = low + blocks * CH
-                lead, trail = rows_ref[low : low + CH, :], rows_ref[high : high + CH, :]
-                lead, trail = cos_in * lead + sin_in * trail, cos_in * trail - sin_in * lead
-                lead, trail = lead + lead * lax.erf(lead), trail + trail * lax.erf(trail)
-                yt_ref[low : low + CH, :] = (cos_out * lead - sin_out * trail).astype(BF16)
-                yt_ref[high : high + CH, :] = (cos_out * trail + sin_out * lead).astype(BF16)
+    def lanes_of(rows, ref, *lead):
+        return jnp.concatenate(
+            [ref[(*lead, pl.ds(row + part, 1), slice(None))] for row in rows for part in range(per_step)], axis=1
+        )
+
+    def gather(rows, part):
+        kept = slice(part * HALF, (part + 1) * HALF if part == 0 else COLS)
+        for half, row in enumerate(rows):
+            tile = jnp.minimum(row // ROWS, SLICES - 1)
+            one_src = (src_ids == lanes_of([row], src_ref)).astype(F32).astype(BF16)
+            rows_ref[kept, half * STEP : (half + 1) * STEP] = jnp.dot(
+                xt_ref[tile, kept, :], one_src, preferred_element_type=F32
+            )
+
+    def convert(rows, order):
+        offset, blocks = SPANS[order]
+        if order == 0:
+            scale = lanes_of(rows, coef_ref, 16)
+            for low in range(0, blocks * CH, CH):
+                gathered = rows_ref[low : low + CH, :]
+                yt_ref[low : low + CH, :] = ((gathered + gathered * lax.erf(gathered)) * scale).astype(BF16)
+            return
+        cos_in, sin_in, cos_out, sin_out = (lanes_of(rows, coef_ref, 4 * (order - 1) + part) for part in range(4))
+        for block in range(blocks):
+            low = (offset + block) * CH
+            high = low + blocks * CH
+            lead, trail = rows_ref[low : low + CH, :], rows_ref[high : high + CH, :]
+            lead, trail = cos_in * lead + sin_in * trail, cos_in * trail - sin_in * lead
+            lead, trail = lead + lead * lax.erf(lead), trail + trail * lax.erf(trail)
+            yt_ref[low : low + CH, :] = (cos_out * lead - sin_out * trail).astype(BF16)
+            yt_ref[high : high + CH, :] = (cos_out * trail + sin_out * lead).astype(BF16)
+
+    def scatter(rows, part):
+        columns = slice(part * CUT, min((part + 1) * CUT, COLS))
         one_tgt = (tgt_ids == lanes_of(rows, tgt_ref)).astype(F32).astype(BF16)
-        acc_ref[:, :COLS] += lax.dot_general(
-            one_tgt, yt_ref[...], (((1,), (1,)), ((), ())), preferred_element_type=F32
+        acc_ref[:, columns] += lax.dot_general(
+            one_tgt, yt_ref[columns, :], (((1,), (1,)), ((), ())), preferred_element_type=F32
         )
+
+    def two_rows(pair):
+        return [list_ref[2 * pair], list_ref[2 * pair + 1]]
+
+    def one_pair(pair, carry):
+        before, now, then = (two_rows(pair + part) for part in range(3))
+        scatter(before, 0)
+        for order in (4, 3, 2):
+            convert(now, order)
+        gather(then, 1)
+        scatter(now, 1)
+        for order in (0, 1):
+            convert(now, order)
+        gather(then, 0)
         return carry
 
-    lax.fori_loop(0, (steps + 1) // 2, two_steps, 0)
+    for part in range(2):
+        gather(two_rows(1), part)
+    lax.fori_loop(0, pairs, one_pair, 0)
+    scatter(two_rows(pairs), 0)
     for index in range(4):
         out_ref[:, index, :, :] = (
             acc_ref[:, index * LANES : (index + 1) * LANES].reshape(SRC, ROWS, LANES).astype(BF16)
         )
 
+
+def spread_positions(packed):
+    packed = packed.astype(F32)
+    tiles = [packed] + [pltpu.roll(packed, LANES - CH * index, 1) for index in range(1, SLICES)]
+    return jnp.concatenate(tiles, axis=0).astype(BF16)
+
+
+def message_kernel(
+    feats_ref, pos_ref0, pos_ref1, pos_ref2, pos_ref3, kidx_ref, kfilter_ref, parts_ref, out_ref
+):
+    del parts_ref
+    zone = lax.axis_index("zh")
+    piece = lax.axis_index("y") * R + lax.axis_index("r")
+    kslice = SRC * ROWS
+    k_start = pl.multiple_of(piece * kslice, kslice)
     row_ids = lax.broadcasted_iota(jnp.int32, (LANES, kslice), 0)
     k_rows = kidx_ref[:, pl.ds(k_start, kslice)].astype(F32)
     k_table = jnp.zeros((LANES, kslice), F32)
     for axis in range(3):
-        start = POS_LANE + 3 * axis
-        k_table = jnp.where((row_ids >= start) & (row_ids < start + 3), k_rows[axis : axis + 1, :], k_table)
-    atoms = SLICES * TGT * ROWS
-    charges = feats_ref[:, :, 4, :, :].reshape(atoms, LANES)
+        k_table = jnp.where((row_ids >= 3 * axis) & (row_ids < 3 * axis + 3), k_rows[axis : axis + 1, :], k_table)
+    charges = jnp.concatenate(
+        [feats_ref[:, CHARGE_TILE + source, :, :].reshape(TGT * ROWS, LANES) for source in range(SLICES)], axis=0
+    )
     turns = lax.dot_general(
         k_table.T.astype(BF16),
-        feats_ref[:, :, 3, :, :].reshape(atoms, LANES),
+        spread_positions(feats_ref[:, POS_TILE, :, :].reshape(TGT * ROWS, LANES)),
         (((1,), (1,)), ((), ())),
         preferred_element_type=F32,
     )
     own_pos = jnp.concatenate(
-        [ref[...].reshape(SLICES * ROWS, LANES) for ref in (pos_ref0, pos_ref1, pos_ref2, pos_ref3)], axis=0
+        [spread_positions(ref[...]) for ref in (pos_ref0, pos_ref1, pos_ref2, pos_ref3)], axis=0
     )
     own_turns = jnp.dot(own_pos, k_table.astype(BF16), preferred_element_type=F32)
     total = jnp.zeros((kslice, LANES), F32)
@@ -385,14 +455,14 @@
         name="first",
     )(counts, *sources, *weights, k_filter)
     group = lax.all_to_all(group, ("y", "r"), 0, 0)
-    feats_out = (TGT, SLICES, 5, ROWS, LANES)
-    pos_out = (SLICES, ROWS, LANES)
+    feats_out = (TGT, TILES, ROWS, LANES)
+    pos_out = (ROWS, LANES)
     feats, pos = pl.pallas_call(
         spread_kernel,
         out_shape=(jax.ShapeDtypeStruct(feats_out, BF16), jax.ShapeDtypeStruct(pos_out, BF16)),
         in_specs=[vmem],
         out_specs=(hbm, vmem),
-        scratch_shapes=[pltpu.SemaphoreType.DMA((TGT,))],
+        scratch_shapes=[pltpu.VMEM(feats_out[1:], BF16), pltpu.SemaphoreType.DMA((TGT,))],
         compiler_params=params(32),
         cost_estimate=COST["spread"],
         name="spread",
@@ -406,7 +476,7 @@
     parts = pl.pallas_call(
         main_kernel,
         out_shape=jax.ShapeDtypeStruct(parts_out, BF16),
-        in_specs=[smem, hbm] + [vmem] * 7,
+        in_specs=[smem, hbm, vmem],
         out_specs=vmem,
         scratch_shapes=[
             pltpu.VMEM(feats_out, BF16),
@@ -417,13 +487,23 @@
             pltpu.VMEM((COLS, 2 * STEP), F32),
             pltpu.VMEM((COLS, 2 * STEP), BF16),
             pltpu.VMEM((kslice, 4 * LANES), F32),
-            pltpu.SMEM((SLICES * (slots // STEP) + 1,), jnp.int32),
+            pltpu.SMEM((SLICES * (slots // STEP) + 5,), jnp.int32),
             pltpu.SemaphoreType.DMA((1,)),
         ],
         compiler_params=params(32),
         cost_estimate=COST["edge_sums"],
         name="edge_sums",
-    )(counts, feats, group, *zones, k_index, k_filter)
+    )(counts, feats, group)
+    parts = pl.pallas_call(
+        message_kernel,
+        out_shape=jax.ShapeDtypeStruct(parts_out, BF16),
+        in_specs=[vmem] * 8,
+        out_specs=vmem,
+        input_output_aliases={7: 0},
+        compiler_params=params(32),
+        cost_estimate=COST["message"],
+        name="message",
+    )(feats, *zones, k_index, k_filter, parts)
     parts = lax.all_to_all(parts, SRC_AXES, 0, 0)
 
     norm = 1.0 / math.sqrt(SRC * TGT * ROWS * k_index.shape[1])

time: 66.1 us -> 64.1 us (0.970)
  waiting for transfers between devices: 3.54 us -> 1.67 us
  Pallas kernels: 12.7 us -> 12 us
    ppermute x3, waiting for transfers between devices: 3.54 us -> 0.01 us  [body(): lax.ppermute(pos, 'zh', [(i, (i + shift) % ZH) for i in range(ZH)])]
    pallas_call x1, Pallas kernels: 6.57 us -> 4.53 us  [body(): pl.pallas_call(main_kernel, out_shape=jax.ShapeDtypeStruct(parts_out, BF1...]
    all_to_all x1, waiting for transfers between devices: 0.01 us -> 1.66 us  [body(): feats = lax.all_to_all(feats, 'tgt', 0, 0)]
    pallas_call x0 -> x1, Pallas kernels: none -> 1.19 us  [body(): pl.pallas_call(message_kernel, out_shape=jax.ShapeDtypeStruct(parts_out,...]
  transfers between devices with their start and end apart: 4 -> 4, of which waited for: 1 -> 1; matrix products, arithmetic and copies ran while one was open for 0% -> 0% of each run, Pallas kernels for 0% -> 7%
where the time goes in v1:
time: 64.1 us; the launch traced here: 63.7 us
  blocking collectives  35 us (55%)
  starting transfers between devices  14.3 us (22%)
  Pallas kernels  12 us (19%)
  waiting for transfers between devices  1.67 us (3%)
  between operations  0.79 us (1%)
    all_to_all x1, blocking collectives, body(): parts = lax.all_to_all(parts, SRC_AXES, 0, 0)  23.6 us
    all_to_all x1, blocking collectives, body(): group = lax.all_to_all(group, ('y', 'r'), 0, 0)  11.4 us
    ppermute x3, starting transfers between devices, body(): lax.ppermute(pos, 'zh', [(i, (i + shift) % ZH) for i in range(ZH)])  8.74 us
    all_to_all x1, starting transfers between devices, body(): feats = lax.all_to_all(feats, 'tgt', 0, 0)  5.57 us
    pallas_call x1, Pallas kernels, body(): pl.pallas_call(main_kernel, out_shape=jax.ShapeDtypeStruct(parts_out, BF1...  4.53 us
    pallas_call x1, Pallas kernels, body(): pl.pallas_call(first_kernel, out_shape=(jax.ShapeDtypeStruct(group_out, B...  4.09 us
    all_to_all x1, waiting for transfers between devices, body(): feats = lax.all_to_all(feats, 'tgt', 0, 0)  1.66 us
  transfers between devices with their start and end apart: 4, of which 1 were waited for; matrix products, arithmetic and copies ran while one was open for 0% of the time, Pallas kernels for 7%

profile of v1, /device:TPU:1, one launch (start us, length us, event | category | flops | bytes accessed | tf_op | source)
XLA Modules:
  0.0 63.7 jit_solution(12451020291222434780)
XLA Ops:
  0.6 0.0 copy-start.5
  0.6 4.1 %first.1 = (bf16[8,10,8,128]{3,2,1,0:T(8,128)(2,1)}, f32[256,128]{1,0:T(8,128)}) custom-call(s32[8,32]{1,0:T(8,128)} %bitcast.5, bf16[8,3200]{1,0:T(8,128)(2,1)} %refs_0_.1, f32[3,8]{1,0:T(4,128)} %refs_1_.2, s32[8,128]{1,0:T(8,128)} %bitcast.7, s32[8,128]{1,0:T(8,128)} %bitcast.8, f32[8,128]{1,0:T(8,128)} %bitcast.9, f32[8,128]{1,0:T(8,128)} %bitcast.10, ...), custom_call_target="tpu_custom_call" | custom-call | flops 50000000 | bytes 3000000 | tf_op jit(solution)/shard_map/first/pallas_call | solution.py:445
  4.7 11.4 %all_to_all.15.parts_ref.group_ref = bf16[8,10,8,128]{3,2,1,0:T(8,128)(2,1)S(1)} all-to-all(bf16[8,10,8,128]{3,2,1,0:T(8,128)(2,1)} %get-tuple-element.6), channel_id=1, replica_groups=mesh['y'=2,'zh'=4,'r'=4,'tgt'=8] {'y','r'}, dimensions={0} | all-to-all | bytes 327680 | tf_op jit(solution)/shard_map/all_to_all | solution.py:457
  16.1 1.0 %spread.1 = (bf16[8,34,8,128]{3,2,1,0:T(8,128)(2,1)}, bf16[8,128]{1,0:T(8,128)(2,1)S(1)}) custom-call(bf16[8,10,8,128]{3,2,1,0:T(8,128)(2,1)S(1)} %all_to_all.15.parts_ref.group_ref), custom_call_target="tpu_custom_call" | custom-call | bytes 800000 | tf_op jit(solution)/shard_map/spread/pallas_call | solution.py:460
  17.1 5.6 %all-to-all-start.1 = ((bf16[8,34,8,128]{3,2,1,0:T(8,128)(2,1)}), bf16[8,34,8,128]{3,2,1,0:T(8,128)(2,1)S(1)}, u32[]{:S(2)}, u32[]{:S(2)}) async-start(bf16[8,34,8,128]{3,2,1,0:T(8,128)(2,1)} %get-tuple-element.7), calls=%async_computation.1 | async-start | bytes 1114112 | tf_op jit(solution)/shard_map/all_to_all | solution.py:470
  22.7 0.0 copy-start.6
  22.7 0.0 copy-start.7
  22.7 5.5 %collective-permute-start.2 = (bf16[8,128]{1,0:T(8,128)(2,1)S(1)}, bf16[8,128]{1,0:T(8,128)(2,1)S(1)}, u32[]{:S(2)}, u32[]{:S(2)}) collective-permute-start(bf16[8,128]{1,0:T(8,128)(2,1)S(1)} %get-tuple-element.8.pos_ref0), channel_id=1, source_target_pairs={{0,96},{32,0},{64,32},{96,64},{1,97},{33,1},{65,33},{97,65},{2,98}... | collective-permute-start | bytes 6152 | tf_op jit(solution)/shard_map/ppermute | solution.py:473
  28.2 1.0 %collective-permute-start.1 = (bf16[8,128]{1,0:T(8,128)(2,1)S(1)}, bf16[8,128]{1,0:T(8,128)(2,1)S(1)}, u32[]{:S(2)}, u32[]{:S(2)}) collective-permute-start(bf16[8,128]{1,0:T(8,128)(2,1)S(1)} %get-tuple-element.8.pos_ref0), channel_id=1, source_target_pairs={{0,64},{32,96},{64,0},{96,32},{1,65},{33,97},{65,1},{97,33},{2,66}... | collective-permute-start | bytes 6152 | tf_op jit(solution)/shard_map/ppermute | solution.py:473
  29.1 2.3 %collective-permute-start = (bf16[8,128]{1,0:T(8,128)(2,1)S(1)}, bf16[8,128]{1,0:T(8,128)(2,1)S(1)}, u32[]{:S(2)}, u32[]{:S(2)}) collective-permute-start(bf16[8,128]{1,0:T(8,128)(2,1)S(1)} %get-tuple-element.8.pos_ref0), channel_id=1, source_target_pairs={{0,32},{32,64},{64,96},{96,0},{1,33},{33,65},{65,97},{97,1},{2,34}... | collective-permute-start | bytes 6152 | tf_op jit(solution)/shard_map/ppermute | solution.py:473
  31.4 1.7 %all-to-all-done.1.feats_hbm.feats_ref = bf16[8,34,8,128]{3,2,1,0:T(8,128)(2,1)S(1)} async-done(((bf16[8,34,8,128]{3,2,1,0:T(8,128)(2,1)}), bf16[8,34,8,128]{3,2,1,0:T(8,128)(2,1)S(1)}, u32[]{:S(2)}, u32[]{:S(2)}) %all-to-all-start.1) | async-done | bytes 557088 | tf_op jit(solution)/shard_map/all_to_all | solution.py:470
  33.1 0.0 copy-done.5
  33.1 4.5 %edge_sums.1.parts_ref = bf16[32,5,8,128]{3,2,1,0:T(8,128)(2,1)S(1)} custom-call(s32[8,32]{1,0:T(8,128)S(1)} %bitcast.6, bf16[8,34,8,128]{3,2,1,0:T(8,128)(2,1)S(1)} %all-to-all-done.1.feats_hbm.feats_ref, bf16[8,10,8,128]{3,2,1,0:T(8,128)(2,1)S(1)} %all_to_all.15.parts_ref.group_ref), custom_call_target="tpu_custom_call" | custom-call | flops 8000000000 | bytes 2000000 | tf_op jit(solution)/shard_map/edge_sums/pallas_call | solution.py:476
  37.6 0.0 collective-permute-done.2.pos_ref3
  37.6 0.0 collective-permute-done.1.pos_ref2
  37.6 0.0 collective-permute-done.pos_ref1
  37.7 0.0 copy-done.6
  37.7 0.0 copy-done.7
  37.7 0.0 copy-start
  37.7 0.0 copy-start.1
  37.7 0.0 copy-start.2
  37.7 0.0 copy-start.3
  37.7 0.0 copy-start.4
  37.7 1.2 %message.1 = bf16[32,5,8,128]{3,2,1,0:T(8,128)(2,1)S(1)} custom-call(bf16[8,34,8,128]{3,2,1,0:T(8,128)(2,1)S(1)} %all-to-all-done.1.feats_hbm.feats_ref, bf16[8,128]{1,0:T(8,128)(2,1)S(1)} %get-tuple-element.8.pos_ref0, bf16[8,128]{1,0:T(8,128)(2,1)S(1)} %collective-permute-done.pos_ref1, ...), custom_call_target="tpu_custom_call", output_to_operand_aliasing={{}: (7, {})} | custom-call | flops 3000000000 | bytes 1000000 | tf_op jit(solution)/shard_map/message/pallas_call | solution.py:497
  38.9 23.6 %all_to_all.16.refs_0_ = bf16[32,5,8,128]{3,2,1,0:T(8,128)(2,1)S(1)} all-to-all(bf16[32,5,8,128]{3,2,1,0:T(8,128)(2,1)S(1)} %message.1), channel_id=1, replica_groups=mesh['y'=2,'zh'=4,'r'=4,'tgt'=8] {'y','zh','r'}, dimensions={0} | all-to-all | bytes 655360 | tf_op jit(solution)/shard_map/all_to_all | solution.py:507
  62.5 0.0 copy-done
  62.5 0.0 copy-done.1
  62.5 0.0 copy-done.2
  62.5 0.0 copy-done.3
  62.5 0.0 copy-done.4
  62.5 1.2 %last_conv.1 = (bf16[8,3200]{1,0:T(8,128)(2,1)}, f32[8,128]{1,0:T(8,128)}) custom-call(bf16[32,5,8,128]{3,2,1,0:T(8,128)(2,1)S(1)} %all_to_all.16.refs_0_, bf16[2,640,640]{2,1,0:T(8,128)(2,1)S(1)} %copy-done.1, bf16[2,2,512,512]{3,2,1,0:T(8,128)(2,1)S(1)} %copy-done, bf16[2,2,384,384]{3,2,1,0:T(8,128)(2,1)S(1)} %copy-done.2, ...), custom_call_target="tpu_custom_call" | custom-call | flops 100000000 | bytes 3200000 | tf_op jit(solution)/shard_map/last_conv/pallas_call | solution.py:510
Async XLA Ops:
  0.6 32.5 %copy-start.5 = (s32[32,8]{0,1:T(8,128)S(1)}, s32[32,8]{0,1:T(8,128)}, u32[]{:S(2)}) copy-start(s32[32,8]{0,1:T(8,128)} %param.20) | copy-start | bytes 3076
  17.1 16.0 %all-to-all-start.1 = ((bf16[8,34,8,128]{3,2,1,0:T(8,128)(2,1)}), bf16[8,34,8,128]{3,2,1,0:T(8,128)(2,1)S(1)}, u32[]{:S(2)}, u32[]{:S(2)}) async-start(bf16[8,34,8,128]{3,2,1,0:T(8,128)(2,1)} %get-tuple-element.7), calls=%async_computation.1 | async-start | bytes 1114112 | tf_op jit(solution)/shard_map/all_to_all | solution.py:470
  22.7 15.0 %copy-start.6 = (f32[256,128]{1,0:T(8,128)S(1)}, f32[256,128]{1,0:T(8,128)}, u32[]{:S(2)}) copy-start(f32[256,128]{1,0:T(8,128)} %get-tuple-element.9.kfilter_ref) | copy-start | bytes 393220
  22.7 15.0 %copy-start.7 = (s32[3,2048]{1,0:T(4,128)S(1)}, s32[3,2048]{1,0:T(4,128)}, u32[]{:S(2)}) copy-start(s32[3,2048]{1,0:T(4,128)} %kidx_ref.1) | copy-start | bytes 73732
  22.7 14.9 %collective-permute-start.2 = (bf16[8,128]{1,0:T(8,128)(2,1)S(1)}, bf16[8,128]{1,0:T(8,128)(2,1)S(1)}, u32[]{:S(2)}, u32[]{:S(2)}) collective-permute-start(bf16[8,128]{1,0:T(8,128)(2,1)S(1)} %get-tuple-element.8.pos_ref0), channel_id=1, source_target_pairs={{0,96},{32,0},{64,32},{96,64},{1,97},{33,1},{65,33},{97,65},{2,98}... | collective-permute-start | bytes 6152 | tf_op jit(solution)/shard_map/ppermute | solution.py:473
  28.2 9.5 %collective-permute-start.1 = (bf16[8,128]{1,0:T(8,128)(2,1)S(1)}, bf16[8,128]{1,0:T(8,128)(2,1)S(1)}, u32[]{:S(2)}, u32[]{:S(2)}) collective-permute-start(bf16[8,128]{1,0:T(8,128)(2,1)S(1)} %get-tuple-element.8.pos_ref0), channel_id=1, source_target_pairs={{0,64},{32,96},{64,0},{96,32},{1,65},{33,97},{65,1},{97,33},{2,66}... | collective-permute-start | bytes 6152 | tf_op jit(solution)/shard_map/ppermute | solution.py:473
  29.1 8.5 %collective-permute-start = (bf16[8,128]{1,0:T(8,128)(2,1)S(1)}, bf16[8,128]{1,0:T(8,128)(2,1)S(1)}, u32[]{:S(2)}, u32[]{:S(2)}) collective-permute-start(bf16[8,128]{1,0:T(8,128)(2,1)S(1)} %get-tuple-element.8.pos_ref0), channel_id=1, source_target_pairs={{0,32},{32,64},{64,96},{96,0},{1,33},{33,65},{65,97},{97,1},{2,34}... | collective-permute-start | bytes 6152 | tf_op jit(solution)/shard_map/ppermute | solution.py:473
  37.7 24.8 %copy-start = (bf16[2,2,512,512]{3,2,1,0:T(8,128)(2,1)S(1)}, bf16[2,2,512,512]{3,2,1,0:T(8,128)(2,1)}, u32[]{:S(2)}) copy-start(bf16[2,2,512,512]{3,2,1,0:T(8,128)(2,1)} %refs_2_.1) | copy-start | bytes 6291460
  37.7 24.8 %copy-start.1 = (bf16[2,640,640]{2,1,0:T(8,128)(2,1)S(1)}, bf16[2,640,640]{2,1,0:T(8,128)(2,1)}, u32[]{:S(2)}) copy-start(bf16[2,640,640]{2,1,0:T(8,128)(2,1)} %refs_1_.3) | copy-start | bytes 4915204
  37.7 24.8 %copy-start.2 = (bf16[2,2,384,384]{3,2,1,0:T(8,128)(2,1)S(1)}, bf16[2,2,384,384]{3,2,1,0:T(8,128)(2,1)}, u32[]{:S(2)}) copy-start(bf16[2,2,384,384]{3,2,1,0:T(8,128)(2,1)} %refs_3_.1) | copy-start | bytes 3538948
  37.7 24.8 %copy-start.3 = (bf16[2,2,256,256]{3,2,1,0:T(8,128)(2,1)S(1)}, bf16[2,2,256,256]{3,2,1,0:T(8,128)(2,1)}, u32[]{:S(2)}) copy-start(bf16[2,2,256,256]{3,2,1,0:T(8,128)(2,1)} %refs_4_.1) | copy-start | bytes 1572868
  37.7 24.8 %copy-start.4 = (bf16[2,2,128,128]{3,2,1,0:T(8,128)(2,1)S(1)}, bf16[2,2,128,128]{3,2,1,0:T(8,128)(2,1)}, u32[]{:S(2)}) copy-start(bf16[2,2,128,128]{3,2,1,0:T(8,128)(2,1)} %refs_5_.1) | copy-start | bytes 393220

commit v2 on v1

--- a/solution.py
+++ b/solution.py
@@ -22,7 +22,10 @@
 CUT = 256
 STEP = 256
 POS_LANE = 16
-LAST_TILE, POS_TILE, CHARGE_TILE, TILES = 24, 25, 26, 34
+MIX_LANE = 32
+HALF_ROW = LANES // 2
+K_SLICES = SLICES // 2
+LAST_TILE, POS_TILE, CHARGE_TILE, TILES = 24, 25, 26, 30
 COST = {
     "first": pl.CostEstimate(flops=50_000_000, transcendentals=0, bytes_accessed=3_000_000),
     "spread": pl.CostEstimate(flops=0, transcendentals=0, bytes_accessed=800_000),
@@ -58,7 +61,7 @@
 
 
 def sincos_turns(turns):
-    part = turns - jnp.floor(turns + 0.5)
+    part = turns - jnp.round(turns)
     x2 = part * part
     s = part * series(SIN_TERMS, x2)
     return 1.0 - s * s, s * series(COS_TERMS, x2)
@@ -112,6 +115,15 @@
     return lead, trail
 
 
+def k_slice_index():
+    return lax.axis_index("y") * (R // 2) + lax.axis_index("r") // 2
+
+
+def in_mix(value):
+    lane = lax.broadcasted_iota(jnp.int32, value.shape, value.ndim - 1)
+    return jnp.where((lane >= MIX_LANE) & (lane < MIX_LANE + HALF_ROW), value, 0.0)
+
+
 def first_kernel(count_ref, *refs):
     sources, kfilter_hbm, (out_ref, kslice_ref) = refs[:11], refs[11], refs[12:14]
     held, (conv_ref, sems) = refs[14:25], refs[25:]
@@ -122,22 +134,22 @@
     for copy in copies:
         copy.start()
     kslice = kslice_ref.shape[0]
-    k_start = pl.multiple_of((lax.axis_index("y") * R + lax.axis_index("r")) * kslice, kslice)
+    k_start = pl.multiple_of(k_slice_index() * kslice, kslice)
     copies.append(pltpu.make_async_copy(kfilter_hbm.at[pl.ds(k_start, kslice), :], kslice_ref, sems.at[11]))
     copies[11].start()
     feats_ref, pos_ref = held[0], held[1]
     for copy in copies[:6]:
         copy.wait()
     pos = position_tile(pos_ref)
-    out_ref[:, 4, :, :] = jnp.broadcast_to(feats_ref[:, :LANES][None], (SLICES, ROWS, LANES))
     for index, tile in enumerate(edge_tiles(count_ref, *held[2:6])):
-        out_ref[:, 5 + index, :, :] = jnp.broadcast_to(tile.astype(BF16)[None], (SLICES, ROWS, LANES))
+        out_ref[:, 4 + index, :, :] = jnp.broadcast_to(tile.astype(BF16)[None], (SLICES, ROWS, LANES))
     x = feats_ref[...].astype(F32)
+    mixed = [pos + in_mix(pltpu.roll(x[:, :LANES], (MIX_LANE - HALF_ROW * half) % LANES, 1)) for half in range(2)]
     place = lax.broadcasted_iota(jnp.int32, (ROWS, LANES), 1) // CH
 
     def emit(tile_index):
         for piece in range(SLICES):
-            tile = pos if tile_index == 3 else jnp.zeros((ROWS, LANES), F32)
+            tile = mixed[piece % 2] if tile_index == 3 else jnp.zeros((ROWS, LANES), F32)
             for within in range(min(8, BLOCKS - 8 * tile_index)):
                 block = 8 * tile_index + within
                 moved = conv_ref[:, block * LANES : (block + 1) * LANES]
@@ -179,7 +191,11 @@
     pos_ref[...] = pos
     for source in range(SLICES):
         held_ref[3 * source : 3 * source + 3, :, :] = parts_ref[source, :3, :, :]
-        held_ref[CHARGE_TILE + source, :, :] = parts_ref[source, 4, :, :]
+    lane = lax.broadcasted_iota(jnp.int32, (ROWS, LANES), 1)
+    for pair in range(SLICES // 2):
+        left = pltpu.roll(mixed[2 * pair], LANES - MIX_LANE, 1)
+        right = pltpu.roll(mixed[2 * pair + 1], HALF_ROW - MIX_LANE, 1)
+        held_ref[CHARGE_TILE + pair, :, :] = jnp.where(lane < HALF_ROW, left, right).astype(BF16)
     held_ref[LAST_TILE, :, :] = group_lanes(mixed, 0)
     held_ref[POS_TILE, :, :] = pos
     copies = [pltpu.make_async_copy(held_ref, out_hbm.at[index], sems.at[index]) for index in range(TGT)]
@@ -217,10 +233,10 @@
         coef_ref[index, spare, :] = jnp.zeros((ROWS, LANES), F32)
     for tile in range(SLICES):
         rows = pl.ds(ROWS * tile, ROWS)
-        src_ref[rows, :] = group_ref[tile, 5, :, :].astype(F32)
-        tgt_ref[rows, :] = group_ref[tile, 6, :, :].astype(F32)
-        angle = group_ref[tile, 7, :, :].astype(F32) + group_ref[tile, 8, :, :].astype(F32)
-        scale = group_ref[tile, 9, :, :].astype(F32) * math.sqrt(0.5)
+        src_ref[rows, :] = group_ref[tile, 4, :, :].astype(F32)
+        tgt_ref[rows, :] = group_ref[tile, 5, :, :].astype(F32)
+        angle = group_ref[tile, 6, :, :].astype(F32) + group_ref[tile, 7, :, :].astype(F32)
+        scale = group_ref[tile, 8, :, :].astype(F32) * math.sqrt(0.5)
         c1, s1 = sincos_turns(angle * (0.5 / math.pi))
         c, s = c1, s1
         coef_ref[16, rows, :] = scale
@@ -261,7 +277,7 @@
     acc_ref[...] = jnp.zeros_like(acc_ref)
     yt_ref[...] = jnp.zeros_like(yt_ref)
     src_ids = lax.broadcasted_iota(jnp.int32, (TGT * ROWS, STEP), 0).astype(F32)
-    tgt_ids = lax.broadcasted_iota(jnp.int32, (SRC * ROWS, 2 * STEP), 0).astype(F32)
+    tgt_ids = lax.broadcasted_iota(jnp.int32, (SRC * ROWS, 2 * STEP), 0).astype(F32).astype(BF16)
 
     def lanes_of(rows, ref, *lead):
         return jnp.concatenate(
@@ -297,7 +313,7 @@
 
     def scatter(rows, part):
         columns = slice(part * CUT, min((part + 1) * CUT, COLS))
-        one_tgt = (tgt_ids == lanes_of(rows, tgt_ref)).astype(F32).astype(BF16)
+        one_tgt = jnp.where(tgt_ids == lanes_of(rows, tgt_ref).astype(BF16), jnp.ones((), BF16), jnp.zeros((), BF16))
         acc_ref[:, columns] += lax.dot_general(
             one_tgt, yt_ref[columns, :], (((1,), (1,)), ((), ())), preferred_element_type=F32
         )
@@ -327,58 +343,69 @@
         )
 
 
-def spread_positions(packed):
+EVEN_ODD = (*range(0, SLICES, 2), *range(1, SLICES, 2))
+
+
+def spread_positions(packed, sources):
     packed = packed.astype(F32)
-    tiles = [packed] + [pltpu.roll(packed, LANES - CH * index, 1) for index in range(1, SLICES)]
+    tiles = [pltpu.roll(packed, LANES - CH * index, 1) if index else packed for index in sources]
     return jnp.concatenate(tiles, axis=0).astype(BF16)
 
 
-def message_kernel(
-    feats_ref, pos_ref0, pos_ref1, pos_ref2, pos_ref3, kidx_ref, kfilter_ref, parts_ref, out_ref
-):
-    del parts_ref
+def message_kernel(feats_ref, pos_ref0, pos_ref1, pos_ref2, pos_ref3, kidx_ref, kfilter_ref, parts_ref, out_ref):
     zone = lax.axis_index("zh")
-    piece = lax.axis_index("y") * R + lax.axis_index("r")
-    kslice = SRC * ROWS
-    k_start = pl.multiple_of(piece * kslice, kslice)
+    kslice = kfilter_ref.shape[0]
+    k_start = pl.multiple_of(k_slice_index() * kslice, kslice)
     row_ids = lax.broadcasted_iota(jnp.int32, (LANES, kslice), 0)
     k_rows = kidx_ref[:, pl.ds(k_start, kslice)].astype(F32)
     k_table = jnp.zeros((LANES, kslice), F32)
     for axis in range(3):
         k_table = jnp.where((row_ids >= 3 * axis) & (row_ids < 3 * axis + 3), k_rows[axis : axis + 1, :], k_table)
     charges = jnp.concatenate(
-        [feats_ref[:, CHARGE_TILE + source, :, :].reshape(TGT * ROWS, LANES) for source in range(SLICES)], axis=0
-    )
+        [feats_ref[:, CHARGE_TILE + pair, :, :].reshape(TGT * ROWS, LANES) for pair in range(SLICES // 2)], axis=0
+    )
+    atoms = charges.shape[0]
     turns = lax.dot_general(
         k_table.T.astype(BF16),
-        spread_positions(feats_ref[:, POS_TILE, :, :].reshape(TGT * ROWS, LANES)),
+        spread_positions(feats_ref[:, POS_TILE, :, :].reshape(TGT * ROWS, LANES), EVEN_ODD),
         (((1,), (1,)), ((), ())),
         preferred_element_type=F32,
     )
     own_pos = jnp.concatenate(
-        [spread_positions(ref[...]) for ref in (pos_ref0, pos_ref1, pos_ref2, pos_ref3)], axis=0
+        [spread_positions(ref[...], range(SLICES)) for ref in (pos_ref0, pos_ref1, pos_ref2, pos_ref3)], axis=0
     )
     own_turns = jnp.dot(own_pos, k_table.astype(BF16), preferred_element_type=F32)
-    total = jnp.zeros((kslice, LANES), F32)
+    filters = kfilter_ref[...]
+    filters = jnp.where(lax.axis_index("r") % 2 == 1, pltpu.roll(filters, HALF_ROW, 1), filters)
+    total = jnp.zeros((SRC * ROWS, LANES), F32)
     for table, own_table in zip(sincos_turns(turns), sincos_turns(own_turns)):
-        factors = jnp.dot(table.astype(BF16), charges, preferred_element_type=F32)
+        table = table.astype(BF16)
+        even = jnp.dot(table[:, :atoms], charges, preferred_element_type=F32)
+        odd = jnp.dot(table[:, atoms:], charges, preferred_element_type=F32)
         own_table = own_table.astype(BF16)
-        for part in split2(kfilter_ref[...] * factors):
+        for part in split2(filters * (even + pltpu.roll(odd, HALF_ROW, 1))):
             total = total + jnp.dot(own_table, part, preferred_element_type=F32)
+    total = in_mix(pltpu.roll(total, MIX_LANE, 1))
     for shift in range(ZH):
         from_zone = (zone + ZH - shift) % ZH
         for y in range(Y):
             low = (shift * SLICES + y * R) * ROWS
-            out_ref[pl.ds(y * ZH * R + from_zone * R, R), 4, :, :] = (
-                total[low : low + R * ROWS].reshape(R, ROWS, LANES).astype(BF16)
-            )
+            place = pl.ds(y * ZH * R + from_zone * R, R)
+            out_ref[place, :3, :, :] = parts_ref[place, :3, :, :]
+            out_ref[place, 3, :, :] = (
+                parts_ref[place, 3, :, :].astype(F32) + total[low : low + R * ROWS].reshape(R, ROWS, LANES)
+            ).astype(BF16)
 
 
 def last_conv_kernel(norm, parts_ref, w0, w1, w2, w3, w4, update_ref, long_ref, conv_ref):
-    total = jnp.zeros((ROWS, LANES), F32)
-    for source in range(SRC):
-        total = total + parts_ref[source, 4, :, :].astype(F32)
-    long_ref[...] = total * norm
+    halves = []
+    for half in range(2):
+        total = jnp.zeros((ROWS, LANES), F32)
+        for source in range(half, SRC, 2):
+            total = total + parts_ref[source, 3, :, :].astype(F32)
+        halves.append(pltpu.roll(total, (HALF_ROW * half - MIX_LANE) % LANES, 1))
+    lane = lax.broadcasted_iota(jnp.int32, (ROWS, LANES), 1)
+    long_ref[...] = jnp.where(lane < HALF_ROW, *halves) * norm
     place = lax.broadcasted_iota(jnp.int32, (ROWS, LANES), 1) // CH
     for index in range(4):
         sums = []
@@ -437,11 +464,11 @@
     vmem = pl.BlockSpec(memory_space=pltpu.VMEM)
     hbm = pl.BlockSpec(memory_space=pltpu.HBM)
     counts = edge_count.T
-    group_out = (SLICES, 10, ROWS, LANES)
+    group_out = (SLICES, 9, ROWS, LANES)
     sources = (atom_feats, positions) + tuple(
         value.reshape(tile_shape) for value in (edge_src, edge_tgt, edge_angle, edge_scale)
     )
-    kslice = SRC * ROWS
+    kslice = k_index.shape[1] // K_SLICES
     group, k_filter = pl.pallas_call(
         first_kernel,
         out_shape=(jax.ShapeDtypeStruct(group_out, BF16), jax.ShapeDtypeStruct((kslice, LANES), F32)),
@@ -472,7 +499,7 @@
     for shift in range(1, ZH):
         zones.append(lax.ppermute(pos, "zh", [(i, (i + shift) % ZH) for i in range(ZH)]))
 
-    parts_out = (SRC, 5, ROWS, LANES)
+    parts_out = (SRC, 4, ROWS, LANES)
     parts = pl.pallas_call(
         main_kernel,
         out_shape=jax.ShapeDtypeStruct(parts_out, BF16),
@@ -486,7 +513,7 @@
             pltpu.VMEM((SLICES, COLS, TGT * ROWS), BF16),
             pltpu.VMEM((COLS, 2 * STEP), F32),
             pltpu.VMEM((COLS, 2 * STEP), BF16),
-            pltpu.VMEM((kslice, 4 * LANES), F32),
+            pltpu.VMEM((SRC * ROWS, 4 * LANES), F32),
             pltpu.SMEM((SLICES * (slots // STEP) + 5,), jnp.int32),
             pltpu.SemaphoreType.DMA((1,)),
         ],
@@ -499,7 +526,6 @@
         out_shape=jax.ShapeDtypeStruct(parts_out, BF16),
         in_specs=[vmem] * 8,
         out_specs=vmem,
-        input_output_aliases={7: 0},
         compiler_params=params(32),
         cost_estimate=COST["message"],
         name="message",

time: 64.1 us -> 62.7 us (0.978)
  waiting for transfers between devices: 1.67 us -> 0.26 us
  Pallas kernels: 12 us -> 13 us
  blocking collectives: 35 us -> 34 us
    all_to_all x1, waiting for transfers between devices: 1.66 us -> 0.25 us  [body(): feats = lax.all_to_all(feats, 'tgt', 0, 0)]
    all_to_all x1, blocking collectives: 23.6 us -> 22.8 us  [body(): parts = lax.all_to_all(parts, SRC_AXES, 0, 0)]
    pallas_call x1, Pallas kernels: 1.19 us -> 1.98 us  [body(): pl.pallas_call(message_kernel, out_shape=jax.ShapeDtypeStruct(parts_out,...]
  transfers between devices with their start and end apart: 4 -> 4, of which waited for: 1 -> 1; matrix products, arithmetic and copies ran while one was open for 0% -> 0% of each run, Pallas kernels for 7% -> 8%
where the time goes in v2:
time: 62.7 us; the launch traced here: 62.4 us
  blocking collectives  34 us (54%)
  starting transfers between devices  14.3 us (23%)
  Pallas kernels  13 us (21%)
  between operations  0.78 us (1%)
    all_to_all x1, blocking collectives, body(): parts = lax.all_to_all(parts, SRC_AXES, 0, 0)  22.8 us
    all_to_all x1, blocking collectives, body(): group = lax.all_to_all(group, ('y', 'r'), 0, 0)  11.2 us
    ppermute x3, starting transfers between devices, body(): lax.ppermute(pos, 'zh', [(i, (i + shift) % ZH) for i in range(ZH)])  8.73 us
    all_to_all x1, starting transfers between devices, body(): feats = lax.all_to_all(feats, 'tgt', 0, 0)  5.57 us
    pallas_call x1, Pallas kernels, body(): pl.pallas_call(main_kernel, out_shape=jax.ShapeDtypeStruct(parts_out, BF1...  4.77 us
    pallas_call x1, Pallas kernels, body(): pl.pallas_call(first_kernel, out_shape=(jax.ShapeDtypeStruct(group_out, B...  4.12 us
    pallas_call x1, Pallas kernels, body(): pl.pallas_call(message_kernel, out_shape=jax.ShapeDtypeStruct(parts_out,...  1.98 us
  transfers between devices with their start and end apart: 4, of which 1 were waited for; matrix products, arithmetic and copies ran while one was open for 0% of the time, Pallas kernels for 8%

profile of v2, /device:TPU:1, one launch (start us, length us, event | category | flops | bytes accessed | tf_op | source)
XLA Modules:
  0.0 62.4 jit_solution(16931902892308097848)
XLA Ops:
  0.6 0.0 copy-start.5
  0.6 4.1 %first.1 = (bf16[8,9,8,128]{3,2,1,0:T(8,128)(2,1)}, f32[512,128]{1,0:T(8,128)}) custom-call(s32[8,32]{1,0:T(8,128)} %bitcast.5, bf16[8,3200]{1,0:T(8,128)(2,1)} %refs_0_.1, f32[3,8]{1,0:T(4,128)} %refs_1_.2, s32[8,128]{1,0:T(8,128)} %bitcast.7, s32[8,128]{1,0:T(8,128)} %bitcast.8, f32[8,128]{1,0:T(8,128)} %bitcast.9, f32[8,128]{1,0:T(8,128)} %bitcast.10, ...), custom_call_target="tpu_custom_call" | custom-call | flops 50000000 | bytes 3000000 | tf_op jit(solution)/shard_map/first/pallas_call | solution.py:472
  4.8 11.2 %all_to_all.15.parts_ref.group_ref = bf16[8,9,8,128]{3,2,1,0:T(8,128)(2,1)S(1)} all-to-all(bf16[8,9,8,128]{3,2,1,0:T(8,128)(2,1)} %get-tuple-element.6), channel_id=1, replica_groups=mesh['y'=2,'zh'=4,'r'=4,'tgt'=8] {'y','r'}, dimensions={0} | all-to-all | bytes 294912 | tf_op jit(solution)/shard_map/all_to_all | solution.py:484
  16.0 0.9 %spread.1 = (bf16[8,30,8,128]{3,2,1,0:T(8,128)(2,1)}, bf16[8,128]{1,0:T(8,128)(2,1)S(1)}) custom-call(bf16[8,9,8,128]{3,2,1,0:T(8,128)(2,1)S(1)} %all_to_all.15.parts_ref.group_ref), custom_call_target="tpu_custom_call" | custom-call | bytes 800000 | tf_op jit(solution)/shard_map/spread/pallas_call | solution.py:487
  16.9 5.6 %all-to-all-start.1 = ((bf16[8,30,8,128]{3,2,1,0:T(8,128)(2,1)}), bf16[8,30,8,128]{3,2,1,0:T(8,128)(2,1)S(1)}, u32[]{:S(2)}, u32[]{:S(2)}) async-start(bf16[8,30,8,128]{3,2,1,0:T(8,128)(2,1)} %get-tuple-element.7), calls=%async_computation.1 | async-start | bytes 983040 | tf_op jit(solution)/shard_map/all_to_all | solution.py:497
  22.5 0.0 copy-start.6
  22.5 0.0 copy-start.7
  22.5 5.5 %collective-permute-start.2 = (bf16[8,128]{1,0:T(8,128)(2,1)S(1)}, bf16[8,128]{1,0:T(8,128)(2,1)S(1)}, u32[]{:S(2)}, u32[]{:S(2)}) collective-permute-start(bf16[8,128]{1,0:T(8,128)(2,1)S(1)} %get-tuple-element.8.pos_ref0), channel_id=1, source_target_pairs={{0,96},{32,0},{64,32},{96,64},{1,97},{33,1},{65,33},{97,65},{2,98}... | collective-permute-start | bytes 6152 | tf_op jit(solution)/shard_map/ppermute | solution.py:500
  28.0 1.0 %collective-permute-start.1 = (bf16[8,128]{1,0:T(8,128)(2,1)S(1)}, bf16[8,128]{1,0:T(8,128)(2,1)S(1)}, u32[]{:S(2)}, u32[]{:S(2)}) collective-permute-start(bf16[8,128]{1,0:T(8,128)(2,1)S(1)} %get-tuple-element.8.pos_ref0), channel_id=1, source_target_pairs={{0,64},{32,96},{64,0},{96,32},{1,65},{33,97},{65,1},{97,33},{2,66}... | collective-permute-start | bytes 6152 | tf_op jit(solution)/shard_map/ppermute | solution.py:500
  29.0 2.3 %collective-permute-start = (bf16[8,128]{1,0:T(8,128)(2,1)S(1)}, bf16[8,128]{1,0:T(8,128)(2,1)S(1)}, u32[]{:S(2)}, u32[]{:S(2)}) collective-permute-start(bf16[8,128]{1,0:T(8,128)(2,1)S(1)} %get-tuple-element.8.pos_ref0), channel_id=1, source_target_pairs={{0,32},{32,64},{64,96},{96,0},{1,33},{33,65},{65,97},{97,1},{2,34}... | collective-permute-start | bytes 6152 | tf_op jit(solution)/shard_map/ppermute | solution.py:500
  31.2 0.2 all-to-all-done.1.feats_hbm.feats_ref
  31.5 0.0 copy-done.5
  31.5 4.8 %edge_sums.1.parts_ref = bf16[32,4,8,128]{3,2,1,0:T(8,128)(2,1)S(1)} custom-call(s32[8,32]{1,0:T(8,128)S(1)} %bitcast.6, bf16[8,30,8,128]{3,2,1,0:T(8,128)(2,1)S(1)} %all-to-all-done.1.feats_hbm.feats_ref, bf16[8,9,8,128]{3,2,1,0:T(8,128)(2,1)S(1)} %all_to_all.15.parts_ref.group_ref), custom_call_target="tpu_custom_call" | custom-call | flops 8000000000 | bytes 2000000 | tf_op jit(solution)/shard_map/edge_sums/pallas_call | solution.py:503
  36.3 0.0 collective-permute-done.2.pos_ref3
  36.3 0.0 collective-permute-done.1.pos_ref2
  36.3 0.0 collective-permute-done.pos_ref1
  36.3 0.0 copy-done.6
  36.3 0.0 copy-done.7
  36.3 0.0 copy-start
  36.3 0.0 copy-start.1
  36.3 0.0 copy-start.2
  36.4 0.0 copy-start.3
  36.4 0.0 copy-start.4
  36.4 2.0 %message.1 = bf16[32,4,8,128]{3,2,1,0:T(8,128)(2,1)S(1)} custom-call(bf16[8,30,8,128]{3,2,1,0:T(8,128)(2,1)S(1)} %all-to-all-done.1.feats_hbm.feats_ref, bf16[8,128]{1,0:T(8,128)(2,1)S(1)} %get-tuple-element.8.pos_ref0, bf16[8,128]{1,0:T(8,128)(2,1)S(1)} %collective-permute-done.pos_ref1, bf16[8,128]{1,0:T(8,128)(2,1)S(1)} %collective-permute-done.1.pos_ref2, ...), custom_call_target="tpu_custom_call" | custom-call | flops 3000000000 | bytes 1000000 | tf_op jit(solution)/shard_map/message/pallas_call | solution.py:524
  38.4 22.8 %all_to_all.16.refs_0_ = bf16[32,4,8,128]{3,2,1,0:T(8,128)(2,1)S(1)} all-to-all(bf16[32,4,8,128]{3,2,1,0:T(8,128)(2,1)S(1)} %message.1), channel_id=1, replica_groups=mesh['y'=2,'zh'=4,'r'=4,'tgt'=8] {'y','zh','r'}, dimensions={0} | all-to-all | bytes 524288 | tf_op jit(solution)/shard_map/all_to_all | solution.py:533
  61.2 0.0 copy-done
  61.2 0.0 copy-done.1
  61.2 0.0 copy-done.2
  61.2 0.0 copy-done.3
  61.2 0.0 copy-done.4
  61.2 1.2 %last_conv.1 = (bf16[8,3200]{1,0:T(8,128)(2,1)}, f32[8,128]{1,0:T(8,128)}) custom-call(bf16[32,4,8,128]{3,2,1,0:T(8,128)(2,1)S(1)} %all_to_all.16.refs_0_, bf16[2,640,640]{2,1,0:T(8,128)(2,1)S(1)} %copy-done.1, bf16[2,2,512,512]{3,2,1,0:T(8,128)(2,1)S(1)} %copy-done, bf16[2,2,384,384]{3,2,1,0:T(8,128)(2,1)S(1)} %copy-done.2, ...), custom_call_target="tpu_custom_call" | custom-call | flops 100000000 | bytes 3200000 | tf_op jit(solution)/shard_map/last_conv/pallas_call | solution.py:536
Async XLA Ops:
  0.6 30.9 %copy-start.5 = (s32[32,8]{0,1:T(8,128)S(1)}, s32[32,8]{0,1:T(8,128)}, u32[]{:S(2)}) copy-start(s32[32,8]{0,1:T(8,128)} %param.20) | copy-start | bytes 3076
  16.9 14.6 %all-to-all-start.1 = ((bf16[8,30,8,128]{3,2,1,0:T(8,128)(2,1)}), bf16[8,30,8,128]{3,2,1,0:T(8,128)(2,1)S(1)}, u32[]{:S(2)}, u32[]{:S(2)}) async-start(bf16[8,30,8,128]{3,2,1,0:T(8,128)(2,1)} %get-tuple-element.7), calls=%async_computation.1 | async-start | bytes 983040 | tf_op jit(solution)/shard_map/all_to_all | solution.py:497
  22.5 13.8 %copy-start.6 = (f32[512,128]{1,0:T(8,128)S(1)}, f32[512,128]{1,0:T(8,128)}, u32[]{:S(2)}) copy-start(f32[512,128]{1,0:T(8,128)} %get-tuple-element.9.kfilter_ref) | copy-start | bytes 786436
  22.5 13.8 %copy-start.7 = (s32[3,2048]{1,0:T(4,128)S(1)}, s32[3,2048]{1,0:T(4,128)}, u32[]{:S(2)}) copy-start(s32[3,2048]{1,0:T(4,128)} %kidx_ref.1) | copy-start | bytes 73732
  22.5 13.8 %collective-permute-start.2 = (bf16[8,128]{1,0:T(8,128)(2,1)S(1)}, bf16[8,128]{1,0:T(8,128)(2,1)S(1)}, u32[]{:S(2)}, u32[]{:S(2)}) collective-permute-start(bf16[8,128]{1,0:T(8,128)(2,1)S(1)} %get-tuple-element.8.pos_ref0), channel_id=1, source_target_pairs={{0,96},{32,0},{64,32},{96,64},{1,97},{33,1},{65,33},{97,65},{2,98}... | collective-permute-start | bytes 6152 | tf_op jit(solution)/shard_map/ppermute | solution.py:500
  28.0 8.3 %collective-permute-start.1 = (bf16[8,128]{1,0:T(8,128)(2,1)S(1)}, bf16[8,128]{1,0:T(8,128)(2,1)S(1)}, u32[]{:S(2)}, u32[]{:S(2)}) collective-permute-start(bf16[8,128]{1,0:T(8,128)(2,1)S(1)} %get-tuple-element.8.pos_ref0), channel_id=1, source_target_pairs={{0,64},{32,96},{64,0},{96,32},{1,65},{33,97},{65,1},{97,33},{2,66}... | collective-permute-start | bytes 6152 | tf_op jit(solution)/shard_map/ppermute | solution.py:500
  29.0 7.3 %collective-permute-start = (bf16[8,128]{1,0:T(8,128)(2,1)S(1)}, bf16[8,128]{1,0:T(8,128)(2,1)S(1)}, u32[]{:S(2)}, u32[]{:S(2)}) collective-permute-start(bf16[8,128]{1,0:T(8,128)(2,1)S(1)} %get-tuple-element.8.pos_ref0), channel_id=1, source_target_pairs={{0,32},{32,64},{64,96},{96,0},{1,33},{33,65},{65,97},{97,1},{2,34}... | collective-permute-start | bytes 6152 | tf_op jit(solution)/shard_map/ppermute | solution.py:500
  36.3 24.8 %copy-start = (bf16[2,2,512,512]{3,2,1,0:T(8,128)(2,1)S(1)}, bf16[2,2,512,512]{3,2,1,0:T(8,128)(2,1)}, u32[]{:S(2)}) copy-start(bf16[2,2,512,512]{3,2,1,0:T(8,128)(2,1)} %refs_2_.1) | copy-start | bytes 6291460
  36.3 24.8 %copy-start.1 = (bf16[2,640,640]{2,1,0:T(8,128)(2,1)S(1)}, bf16[2,640,640]{2,1,0:T(8,128)(2,1)}, u32[]{:S(2)}) copy-start(bf16[2,640,640]{2,1,0:T(8,128)(2,1)} %refs_1_.3) | copy-start | bytes 4915204
  36.3 24.8 %copy-start.2 = (bf16[2,2,384,384]{3,2,1,0:T(8,128)(2,1)S(1)}, bf16[2,2,384,384]{3,2,1,0:T(8,128)(2,1)}, u32[]{:S(2)}) copy-start(bf16[2,2,384,384]{3,2,1,0:T(8,128)(2,1)} %refs_3_.1) | copy-start | bytes 3538948
  36.4 24.8 %copy-start.3 = (bf16[2,2,256,256]{3,2,1,0:T(8,128)(2,1)S(1)}, bf16[2,2,256,256]{3,2,1,0:T(8,128)(2,1)}, u32[]{:S(2)}) copy-start(bf16[2,2,256,256]{3,2,1,0:T(8,128)(2,1)} %refs_4_.1) | copy-start | bytes 1572868
  36.4 24.8 %copy-start.4 = (bf16[2,2,128,128]{3,2,1,0:T(8,128)(2,1)S(1)}, bf16[2,2,128,128]{3,2,1,0:T(8,128)(2,1)}, u32[]{:S(2)}) copy-start(bf16[2,2,128,128]{3,2,1,0:T(8,128)(2,1)} %refs_5_.1) | copy-start | bytes 393220

commit v3 on v2

--- a/solution.py
+++ b/solution.py
@@ -124,23 +124,21 @@
     return jnp.where((lane >= MIX_LANE) & (lane < MIX_LANE + HALF_ROW), value, 0.0)
 
 
-def first_kernel(count_ref, *refs):
-    sources, kfilter_hbm, (out_ref, kslice_ref) = refs[:11], refs[11], refs[12:14]
-    held, (conv_ref, sems) = refs[14:25], refs[25:]
+def first_kernel(count_hbm, *refs):
+    sources, out_ref, held, (conv_ref, count_ref, sems) = refs[:11], refs[11], refs[12:23], refs[23:]
     copies = [
         pltpu.make_async_copy(source if index < 6 else source.at[0], to, sems.at[index])
         for index, (source, to) in enumerate(zip(sources, held))
     ]
+    count_copy = pltpu.make_async_copy(count_hbm, count_ref, sems.at[11])
+    count_copy.start()
     for copy in copies:
         copy.start()
-    kslice = kslice_ref.shape[0]
-    k_start = pl.multiple_of(k_slice_index() * kslice, kslice)
-    copies.append(pltpu.make_async_copy(kfilter_hbm.at[pl.ds(k_start, kslice), :], kslice_ref, sems.at[11]))
-    copies[11].start()
     feats_ref, pos_ref = held[0], held[1]
     for copy in copies[:6]:
         copy.wait()
     pos = position_tile(pos_ref)
+    count_copy.wait()
     for index, tile in enumerate(edge_tiles(count_ref, *held[2:6])):
         out_ref[:, 4 + index, :, :] = jnp.broadcast_to(tile.astype(BF16)[None], (SLICES, ROWS, LANES))
     x = feats_ref[...].astype(F32)
@@ -173,7 +171,6 @@
         conv_ref[:, start + width : start + 2 * width] = root * trail
     for tile_index in range(4):
         emit(tile_index)
-    copies[11].wait()
 
 
 def group_lanes(tiles, first_lane):
@@ -185,28 +182,27 @@
     return packed.astype(BF16)
 
 
-def spread_kernel(parts_ref, out_hbm, pos_ref, held_ref, sems):
+def spread_kernel(parts_ref, out_ref, pos_ref):
+    def put(index, tile):
+        out_ref[:, index, :, :] = jnp.broadcast_to(tile[None], (TGT, ROWS, LANES))
+
     mixed = [parts_ref[source, 3, :, :].astype(F32) for source in range(SLICES)]
     pos = group_lanes(mixed, POS_LANE)
     pos_ref[...] = pos
     for source in range(SLICES):
-        held_ref[3 * source : 3 * source + 3, :, :] = parts_ref[source, :3, :, :]
+        for index in range(3):
+            put(3 * source + index, parts_ref[source, index, :, :])
     lane = lax.broadcasted_iota(jnp.int32, (ROWS, LANES), 1)
     for pair in range(SLICES // 2):
         left = pltpu.roll(mixed[2 * pair], LANES - MIX_LANE, 1)
         right = pltpu.roll(mixed[2 * pair + 1], HALF_ROW - MIX_LANE, 1)
-        held_ref[CHARGE_TILE + pair, :, :] = jnp.where(lane < HALF_ROW, left, right).astype(BF16)
-    held_ref[LAST_TILE, :, :] = group_lanes(mixed, 0)
-    held_ref[POS_TILE, :, :] = pos
-    copies = [pltpu.make_async_copy(held_ref, out_hbm.at[index], sems.at[index]) for index in range(TGT)]
-    for copy in copies:
-        copy.start()
-    for copy in copies:
-        copy.wait()
+        put(CHARGE_TILE + pair, jnp.where(lane < HALF_ROW, left, right).astype(BF16))
+    put(LAST_TILE, group_lanes(mixed, 0))
+    put(POS_TILE, pos)
 
 
 def main_kernel(
-    count_ref,
+    count_hbm,
     feats_hbm,
     group_ref,
     out_ref,
@@ -219,12 +215,15 @@
     yt_ref,
     acc_ref,
     list_ref,
+    count_ref,
     sems,
 ):
     zone = lax.axis_index("zh")
     target_group = lax.axis_index("tgt")
     feats_copy = pltpu.make_async_copy(feats_hbm, feats_ref, sems.at[0])
     feats_copy.start()
+    count_copy = pltpu.make_async_copy(count_hbm, count_ref, sems.at[1])
+    count_copy.start()
 
     spare = pl.ds(ROWS * SLICES, ROWS)
     src_ref[spare, :] = jnp.zeros((ROWS, LANES), F32)
@@ -255,6 +254,7 @@
             xt_ref[tile, index * LANES : (index + 1) * LANES, :] = block.T
         xt_ref[tile, 3 * LANES :, :] = last[tile * CH : (tile + 1) * CH]
 
+    count_copy.wait()
     per_step = STEP // LANES
 
     def list_tile(tile, at):
@@ -354,7 +354,7 @@
 
 def message_kernel(feats_ref, pos_ref0, pos_ref1, pos_ref2, pos_ref3, kidx_ref, kfilter_ref, parts_ref, out_ref):
     zone = lax.axis_index("zh")
-    kslice = kfilter_ref.shape[0]
+    kslice = kfilter_ref.shape[0] // K_SLICES
     k_start = pl.multiple_of(k_slice_index() * kslice, kslice)
     row_ids = lax.broadcasted_iota(jnp.int32, (LANES, kslice), 0)
     k_rows = kidx_ref[:, pl.ds(k_start, kslice)].astype(F32)
@@ -375,7 +375,7 @@
         [spread_positions(ref[...], range(SLICES)) for ref in (pos_ref0, pos_ref1, pos_ref2, pos_ref3)], axis=0
     )
     own_turns = jnp.dot(own_pos, k_table.astype(BF16), preferred_element_type=F32)
-    filters = kfilter_ref[...]
+    filters = kfilter_ref[pl.ds(k_start, kslice), :]
     filters = jnp.where(lax.axis_index("r") % 2 == 1, pltpu.roll(filters, HALF_ROW, 1), filters)
     total = jnp.zeros((SRC * ROWS, LANES), F32)
     for table, own_table in zip(sincos_turns(turns), sincos_turns(own_turns)):
@@ -460,7 +460,6 @@
     slots = edge_src.shape[0]
     columns = atom_feats.shape[1]
     tile_shape = (ROWS, slots // ROWS)
-    smem = pl.BlockSpec(memory_space=pltpu.SMEM)
     vmem = pl.BlockSpec(memory_space=pltpu.VMEM)
     hbm = pl.BlockSpec(memory_space=pltpu.HBM)
     counts = edge_count.T
@@ -468,19 +467,18 @@
     sources = (atom_feats, positions) + tuple(
         value.reshape(tile_shape) for value in (edge_src, edge_tgt, edge_angle, edge_scale)
     )
-    kslice = k_index.shape[1] // K_SLICES
-    group, k_filter = pl.pallas_call(
+    group = pl.pallas_call(
         first_kernel,
-        out_shape=(jax.ShapeDtypeStruct(group_out, BF16), jax.ShapeDtypeStruct((kslice, LANES), F32)),
-        in_specs=[smem] + [hbm] * 12,
-        out_specs=(vmem, vmem),
+        out_shape=jax.ShapeDtypeStruct(group_out, BF16),
+        in_specs=[hbm] * 12,
+        out_specs=vmem,
         scratch_shapes=[pltpu.VMEM(value.shape, value.dtype) for value in sources]
         + [pltpu.VMEM(weight.shape[1:], weight.dtype) for weight in weights]
-        + [pltpu.VMEM((ROWS, columns), F32), pltpu.SemaphoreType.DMA((12,))],
+        + [pltpu.VMEM((ROWS, columns), F32), pltpu.SMEM(counts.shape, jnp.int32), pltpu.SemaphoreType.DMA((12,))],
         compiler_params=params(56),
         cost_estimate=COST["first"],
         name="first",
-    )(counts, *sources, *weights, k_filter)
+    )(counts, *sources, *weights)
     group = lax.all_to_all(group, ("y", "r"), 0, 0)
     feats_out = (TGT, TILES, ROWS, LANES)
     pos_out = (ROWS, LANES)
@@ -488,8 +486,7 @@
         spread_kernel,
         out_shape=(jax.ShapeDtypeStruct(feats_out, BF16), jax.ShapeDtypeStruct(pos_out, BF16)),
         in_specs=[vmem],
-        out_specs=(hbm, vmem),
-        scratch_shapes=[pltpu.VMEM(feats_out[1:], BF16), pltpu.SemaphoreType.DMA((TGT,))],
+        out_specs=(vmem, vmem),
         compiler_params=params(32),
         cost_estimate=COST["spread"],
         name="spread",
@@ -503,7 +500,7 @@
     parts = pl.pallas_call(
         main_kernel,
         out_shape=jax.ShapeDtypeStruct(parts_out, BF16),
-        in_specs=[smem, hbm, vmem],
+        in_specs=[hbm, hbm, vmem],
         out_specs=vmem,
         scratch_shapes=[
             pltpu.VMEM(feats_out, BF16),
@@ -515,7 +512,8 @@
             pltpu.VMEM((COLS, 2 * STEP), BF16),
             pltpu.VMEM((SRC * ROWS, 4 * LANES), F32),
             pltpu.SMEM((SLICES * (slots // STEP) + 5,), jnp.int32),
-            pltpu.SemaphoreType.DMA((1,)),
+            pltpu.SMEM(counts.shape, jnp.int32),
+            pltpu.SemaphoreType.DMA((2,)),
         ],
         compiler_params=params(32),
         cost_estimate=COST["edge_sums"],

time: 62.7 us -> 61.3 us (0.978)
  Pallas kernels: 13 us -> 11.6 us
    pallas_call x1, Pallas kernels: 4.12 us -> 3.18 us  [body(): pl.pallas_call(first_kernel, out_shape=jax.ShapeDtypeStruct(group_out, BF...]
  transfers between devices with their start and end apart: 4 -> 4, of which waited for: 1 -> 1; matrix products, arithmetic and copies ran while one was open for 0% -> 0% of each run, Pallas kernels for 8% -> 7%
where the time goes in v3:
time: 61.3 us; the launch traced here: 61 us
  blocking collectives  34 us (55%)
  starting transfers between devices  14.3 us (23%)
  Pallas kernels  11.6 us (19%)
  between operations  0.78 us (1%)
    all_to_all x1, blocking collectives, body(): parts = lax.all_to_all(parts, SRC_AXES, 0, 0)  22.8 us
    all_to_all x1, blocking collectives, body(): group = lax.all_to_all(group, ('y', 'r'), 0, 0)  11.2 us
    ppermute x3, starting transfers between devices, body(): lax.ppermute(pos, 'zh', [(i, (i + shift) % ZH) for i in range(ZH)])  8.73 us
    all_to_all x1, starting transfers between devices, body(): feats = lax.all_to_all(feats, 'tgt', 0, 0)  5.56 us
    pallas_call x1, Pallas kernels, body(): pl.pallas_call(main_kernel, out_shape=jax.ShapeDtypeStruct(parts_out, BF1...  4.41 us
    pallas_call x1, Pallas kernels, body(): pl.pallas_call(first_kernel, out_shape=jax.ShapeDtypeStruct(group_out, BF...  3.18 us
    pallas_call x1, Pallas kernels, body(): pl.pallas_call(message_kernel, out_shape=jax.ShapeDtypeStruct(parts_out,...  1.99 us
  transfers between devices with their start and end apart: 4, of which 1 were waited for; matrix products, arithmetic and copies ran while one was open for 0% of the time, Pallas kernels for 7%

profile of v3, /device:TPU:1, one launch (start us, length us, event | category | flops | bytes accessed | tf_op | source)
XLA Modules:
  0.0 61.0 jit_solution(14724320033642523529)
XLA Ops:
  0.6 0.0 copy-start.5
  0.6 3.2 %first.1 = bf16[8,9,8,128]{3,2,1,0:T(8,128)(2,1)} custom-call(s32[8,32]{1,0:T(8,128)} %bitcast.5, bf16[8,3200]{1,0:T(8,128)(2,1)} %refs_0_.1, f32[3,8]{1,0:T(4,128)} %refs_1_.2, s32[8,128]{1,0:T(8,128)} %bitcast.7, s32[8,128]{1,0:T(8,128)} %bitcast.8, f32[8,128]{1,0:T(8,128)} %bitcast.9, f32[8,128]{1,0:T(8,128)} %bitcast.10, bf16[2,640,640]{2,1,0:T(8,128)(2,1)} %refs_1_.3, ...), custom_call_target="tpu_custom_call" | custom-call | flops 50000000 | bytes 3000000 | tf_op jit(solution)/shard_map/first/pallas_call | solution.py:470
  3.8 11.2 %all_to_all.15.parts_ref.group_ref = bf16[8,9,8,128]{3,2,1,0:T(8,128)(2,1)S(1)} all-to-all(bf16[8,9,8,128]{3,2,1,0:T(8,128)(2,1)} %first.1), channel_id=1, replica_groups=mesh['y'=2,'zh'=4,'r'=4,'tgt'=8] {'y','r'}, dimensions={0} | all-to-all | bytes 294912 | tf_op jit(solution)/shard_map/all_to_all | solution.py:482
  15.0 0.9 %spread.1 = (bf16[8,30,8,128]{3,2,1,0:T(8,128)(2,1)}, bf16[8,128]{1,0:T(8,128)(2,1)S(1)}) custom-call(bf16[8,9,8,128]{3,2,1,0:T(8,128)(2,1)S(1)} %all_to_all.15.parts_ref.group_ref), custom_call_target="tpu_custom_call" | custom-call | bytes 800000 | tf_op jit(solution)/shard_map/spread/pallas_call | solution.py:485
  15.9 5.6 %all-to-all-start.1 = ((bf16[8,30,8,128]{3,2,1,0:T(8,128)(2,1)}), bf16[8,30,8,128]{3,2,1,0:T(8,128)(2,1)S(1)}, u32[]{:S(2)}, u32[]{:S(2)}) async-start(bf16[8,30,8,128]{3,2,1,0:T(8,128)(2,1)} %get-tuple-element.4), calls=%async_computation.1 | async-start | bytes 983040 | tf_op jit(solution)/shard_map/all_to_all | solution.py:494
  21.5 0.0 copy-start.6
  21.5 0.0 copy-start.7
  21.5 5.5 %collective-permute-start.2 = (bf16[8,128]{1,0:T(8,128)(2,1)S(1)}, bf16[8,128]{1,0:T(8,128)(2,1)S(1)}, u32[]{:S(2)}, u32[]{:S(2)}) collective-permute-start(bf16[8,128]{1,0:T(8,128)(2,1)S(1)} %get-tuple-element.5.pos_ref0), channel_id=1, source_target_pairs={{0,96},{32,0},{64,32},{96,64},{1,97},{33,1},{65,33},{97,65},{2,98}... | collective-permute-start | bytes 6152 | tf_op jit(solution)/shard_map/ppermute | solution.py:497
  27.0 1.0 %collective-permute-start.1 = (bf16[8,128]{1,0:T(8,128)(2,1)S(1)}, bf16[8,128]{1,0:T(8,128)(2,1)S(1)}, u32[]{:S(2)}, u32[]{:S(2)}) collective-permute-start(bf16[8,128]{1,0:T(8,128)(2,1)S(1)} %get-tuple-element.5.pos_ref0), channel_id=1, source_target_pairs={{0,64},{32,96},{64,0},{96,32},{1,65},{33,97},{65,1},{97,33},{2,66}... | collective-permute-start | bytes 6152 | tf_op jit(solution)/shard_map/ppermute | solution.py:497
  28.0 2.3 %collective-permute-start = (bf16[8,128]{1,0:T(8,128)(2,1)S(1)}, bf16[8,128]{1,0:T(8,128)(2,1)S(1)}, u32[]{:S(2)}, u32[]{:S(2)}) collective-permute-start(bf16[8,128]{1,0:T(8,128)(2,1)S(1)} %get-tuple-element.5.pos_ref0), channel_id=1, source_target_pairs={{0,32},{32,64},{64,96},{96,0},{1,33},{33,65},{65,97},{97,1},{2,34}... | collective-permute-start | bytes 6152 | tf_op jit(solution)/shard_map/ppermute | solution.py:497
  30.2 0.2 all-to-all-done.1.feats_hbm.feats_ref
  30.5 0.0 copy-done.5
  30.5 4.4 %edge_sums.1.parts_ref = bf16[32,4,8,128]{3,2,1,0:T(8,128)(2,1)S(1)} custom-call(s32[8,32]{1,0:T(8,128)S(1)} %bitcast.6, bf16[8,30,8,128]{3,2,1,0:T(8,128)(2,1)S(1)} %all-to-all-done.1.feats_hbm.feats_ref, bf16[8,9,8,128]{3,2,1,0:T(8,128)(2,1)S(1)} %all_to_all.15.parts_ref.group_ref), custom_call_target="tpu_custom_call" | custom-call | flops 8000000000 | bytes 2000000 | tf_op jit(solution)/shard_map/edge_sums/pallas_call | solution.py:500
  34.9 0.0 copy-start.2
  34.9 0.0 copy-start.3
  34.9 0.0 copy-start.4
  34.9 0.0 collective-permute-done.2.pos_ref3
  34.9 0.0 collective-permute-done.1.pos_ref2
  34.9 0.0 collective-permute-done.pos_ref1
  35.0 0.0 copy-done.6
  35.0 0.0 copy-done.7
  35.0 0.0 copy-start
  35.0 0.0 copy-start.1
  35.0 2.0 %message.1 = bf16[32,4,8,128]{3,2,1,0:T(8,128)(2,1)S(1)} custom-call(bf16[8,30,8,128]{3,2,1,0:T(8,128)(2,1)S(1)} %all-to-all-done.1.feats_hbm.feats_ref, bf16[8,128]{1,0:T(8,128)(2,1)S(1)} %get-tuple-element.5.pos_ref0, bf16[8,128]{1,0:T(8,128)(2,1)S(1)} %collective-permute-done.pos_ref1, bf16[8,128]{1,0:T(8,128)(2,1)S(1)} %collective-permute-done.1.pos_ref2, ...), custom_call_target="tpu_custom_call" | custom-call | flops 3000000000 | bytes 1000000 | tf_op jit(solution)/shard_map/message/pallas_call | solution.py:522
  37.0 22.8 %all_to_all.16.refs_0_ = bf16[32,4,8,128]{3,2,1,0:T(8,128)(2,1)S(1)} all-to-all(bf16[32,4,8,128]{3,2,1,0:T(8,128)(2,1)S(1)} %message.1), channel_id=1, replica_groups=mesh['y'=2,'zh'=4,'r'=4,'tgt'=8] {'y','zh','r'}, dimensions={0} | all-to-all | bytes 524288 | tf_op jit(solution)/shard_map/all_to_all | solution.py:531
  59.8 0.0 copy-done.2
  59.8 0.0 copy-done.3
  59.8 0.0 copy-done.4
  59.8 0.0 copy-done
  59.8 0.0 copy-done.1
  59.8 1.2 %last_conv.1 = (bf16[8,3200]{1,0:T(8,128)(2,1)}, f32[8,128]{1,0:T(8,128)}) custom-call(bf16[32,4,8,128]{3,2,1,0:T(8,128)(2,1)S(1)} %all_to_all.16.refs_0_, bf16[2,640,640]{2,1,0:T(8,128)(2,1)S(1)} %copy-done.1, bf16[2,2,512,512]{3,2,1,0:T(8,128)(2,1)S(1)} %copy-done, bf16[2,2,384,384]{3,2,1,0:T(8,128)(2,1)S(1)} %copy-done.2, ...), custom_call_target="tpu_custom_call" | custom-call | flops 100000000 | bytes 3200000 | tf_op jit(solution)/shard_map/last_conv/pallas_call | solution.py:534
Async XLA Ops:
  0.6 29.8 %copy-start.5 = (s32[32,8]{0,1:T(8,128)S(1)}, s32[32,8]{0,1:T(8,128)}, u32[]{:S(2)}) copy-start(s32[32,8]{0,1:T(8,128)} %param.20) | copy-start | bytes 3076
  15.9 14.6 %all-to-all-start.1 = ((bf16[8,30,8,128]{3,2,1,0:T(8,128)(2,1)}), bf16[8,30,8,128]{3,2,1,0:T(8,128)(2,1)S(1)}, u32[]{:S(2)}, u32[]{:S(2)}) async-start(bf16[8,30,8,128]{3,2,1,0:T(8,128)(2,1)} %get-tuple-element.4), calls=%async_computation.1 | async-start | bytes 983040 | tf_op jit(solution)/shard_map/all_to_all | solution.py:494
  21.5 13.5 %copy-start.6 = (f32[2048,128]{1,0:T(8,128)S(1)}, f32[2048,128]{1,0:T(8,128)}, u32[]{:S(2)}) copy-start(f32[2048,128]{1,0:T(8,128)} %kfilter_ref.1) | copy-start | bytes 3145732
  21.5 13.5 %copy-start.7 = (s32[3,2048]{1,0:T(4,128)S(1)}, s32[3,2048]{1,0:T(4,128)}, u32[]{:S(2)}) copy-start(s32[3,2048]{1,0:T(4,128)} %kidx_ref.1) | copy-start | bytes 73732
  21.5 13.4 %collective-permute-start.2 = (bf16[8,128]{1,0:T(8,128)(2,1)S(1)}, bf16[8,128]{1,0:T(8,128)(2,1)S(1)}, u32[]{:S(2)}, u32[]{:S(2)}) collective-permute-start(bf16[8,128]{1,0:T(8,128)(2,1)S(1)} %get-tuple-element.5.pos_ref0), channel_id=1, source_target_pairs={{0,96},{32,0},{64,32},{96,64},{1,97},{33,1},{65,33},{97,65},{2,98}... | collective-permute-start | bytes 6152 | tf_op jit(solution)/shard_map/ppermute | solution.py:497
  27.0 8.0 %collective-permute-start.1 = (bf16[8,128]{1,0:T(8,128)(2,1)S(1)}, bf16[8,128]{1,0:T(8,128)(2,1)S(1)}, u32[]{:S(2)}, u32[]{:S(2)}) collective-permute-start(bf16[8,128]{1,0:T(8,128)(2,1)S(1)} %get-tuple-element.5.pos_ref0), channel_id=1, source_target_pairs={{0,64},{32,96},{64,0},{96,32},{1,65},{33,97},{65,1},{97,33},{2,66}... | collective-permute-start | bytes 6152 | tf_op jit(solution)/shard_map/ppermute | solution.py:497
  28.0 7.0 %collective-permute-start = (bf16[8,128]{1,0:T(8,128)(2,1)S(1)}, bf16[8,128]{1,0:T(8,128)(2,1)S(1)}, u32[]{:S(2)}, u32[]{:S(2)}) collective-permute-start(bf16[8,128]{1,0:T(8,128)(2,1)S(1)} %get-tuple-element.5.pos_ref0), channel_id=1, source_target_pairs={{0,32},{32,64},{64,96},{96,0},{1,33},{33,65},{65,97},{97,1},{2,34}... | collective-permute-start | bytes 6152 | tf_op jit(solution)/shard_map/ppermute | solution.py:497
  34.9 24.9 %copy-start.2 = (bf16[2,2,384,384]{3,2,1,0:T(8,128)(2,1)S(1)}, bf16[2,2,384,384]{3,2,1,0:T(8,128)(2,1)}, u32[]{:S(2)}) copy-start(bf16[2,2,384,384]{3,2,1,0:T(8,128)(2,1)} %refs_3_.1) | copy-start | bytes 3538948
  34.9 24.9 %copy-start.3 = (bf16[2,2,256,256]{3,2,1,0:T(8,128)(2,1)S(1)}, bf16[2,2,256,256]{3,2,1,0:T(8,128)(2,1)}, u32[]{:S(2)}) copy-start(bf16[2,2,256,256]{3,2,1,0:T(8,128)(2,1)} %refs_4_.1) | copy-start | bytes 1572868
  34.9 24.9 %copy-start.4 = (bf16[2,2,128,128]{3,2,1,0:T(8,128)(2,1)S(1)}, bf16[2,2,128,128]{3,2,1,0:T(8,128)(2,1)}, u32[]{:S(2)}) copy-start(bf16[2,2,128,128]{3,2,1,0:T(8,128)(2,1)} %refs_5_.1) | copy-start | bytes 393220
  35.0 24.8 %copy-start = (bf16[2,2,512,512]{3,2,1,0:T(8,128)(2,1)S(1)}, bf16[2,2,512,512]{3,2,1,0:T(8,128)(2,1)}, u32[]{:S(2)}) copy-start(bf16[2,2,512,512]{3,2,1,0:T(8,128)(2,1)} %refs_2_.1) | copy-start | bytes 6291460
  35.0 24.8 %copy-start.1 = (bf16[2,640,640]{2,1,0:T(8,128)(2,1)S(1)}, bf16[2,640,640]{2,1,0:T(8,128)(2,1)}, u32[]{:S(2)}) copy-start(bf16[2,640,640]{2,1,0:T(8,128)(2,1)} %refs_1_.3) | copy-start | bytes 4915204

commit v4 on v3

--- a/solution.py
+++ b/solution.py
@@ -203,10 +203,9 @@
 
 def main_kernel(
     count_hbm,
-    feats_hbm,
+    feats_ref,
     group_ref,
     out_ref,
-    feats_ref,
     src_ref,
     tgt_ref,
     coef_ref,
@@ -216,13 +215,11 @@
     acc_ref,
     list_ref,
     count_ref,
-    sems,
+    sem,
 ):
     zone = lax.axis_index("zh")
     target_group = lax.axis_index("tgt")
-    feats_copy = pltpu.make_async_copy(feats_hbm, feats_ref, sems.at[0])
-    feats_copy.start()
-    count_copy = pltpu.make_async_copy(count_hbm, count_ref, sems.at[1])
+    count_copy = pltpu.make_async_copy(count_hbm, count_ref, sem)
     count_copy.start()
 
     spare = pl.ds(ROWS * SLICES, ROWS)
@@ -246,7 +243,6 @@
             coef_ref[4 * order + 1, rows, :] = s
             coef_ref[4 * order + 2, rows, :] = scale * c
             coef_ref[4 * order + 3, rows, :] = scale * s
-    feats_copy.wait()
     last = feats_ref[:, LAST_TILE, :, :].reshape(TGT * ROWS, LANES).T
     for tile in range(SLICES):
         for index in range(3):
@@ -500,10 +496,9 @@
     parts = pl.pallas_call(
         main_kernel,
         out_shape=jax.ShapeDtypeStruct(parts_out, BF16),
-        in_specs=[hbm, hbm, vmem],
+        in_specs=[hbm, vmem, vmem],
         out_specs=vmem,
         scratch_shapes=[
-            pltpu.VMEM(feats_out, BF16),
             pltpu.VMEM(((SLICES + 1) * ROWS, LANES), F32),
             pltpu.VMEM(((SLICES + 1) * ROWS, LANES), F32),
             pltpu.VMEM((17, (SLICES + 1) * ROWS, LANES), F32),
@@ -513,7 +508,7 @@
             pltpu.VMEM((SRC * ROWS, 4 * LANES), F32),
             pltpu.SMEM((SLICES * (slots // STEP) + 5,), jnp.int32),
             pltpu.SMEM(counts.shape, jnp.int32),
-            pltpu.SemaphoreType.DMA((2,)),
+            pltpu.SemaphoreType.DMA,
         ],
         compiler_params=params(32),
         cost_estimate=COST["edge_sums"],

time: 61.3 us -> 61 us (level)
  no operation moved by 1% of the time
where the time goes in v4:
time: 61 us; the launch traced here: 60.7 us
  blocking collectives  34 us (56%)
  starting transfers between devices  14.3 us (23%)
  Pallas kernels  11.3 us (19%)
  between operations  0.78 us (1%)
    all_to_all x1, blocking collectives, body(): parts = lax.all_to_all(parts, SRC_AXES, 0, 0)  22.8 us
    all_to_all x1, blocking collectives, body(): group = lax.all_to_all(group, ('y', 'r'), 0, 0)  11.2 us
    ppermute x3, starting transfers between devices, body(): lax.ppermute(pos, 'zh', [(i, (i + shift) % ZH) for i in range(ZH)])  8.73 us
    all_to_all x1, starting transfers between devices, body(): feats = lax.all_to_all(feats, 'tgt', 0, 0)  5.56 us
    pallas_call x1, Pallas kernels, body(): pl.pallas_call(main_kernel, out_shape=jax.ShapeDtypeStruct(parts_out, BF1...  4.11 us
    pallas_call x1, Pallas kernels, body(): pl.pallas_call(first_kernel, out_shape=jax.ShapeDtypeStruct(group_out, BF...  3.18 us
    pallas_call x1, Pallas kernels, body(): pl.pallas_call(message_kernel, out_shape=jax.ShapeDtypeStruct(parts_out,...  1.99 us
  transfers between devices with their start and end apart: 4, of which 1 were waited for; matrix products, arithmetic and copies ran while one was open for 0% of the time, Pallas kernels for 7%

profile of v4, /device:TPU:1, one launch (start us, length us, event | category | flops | bytes accessed | tf_op | source)
XLA Modules:
  0.0 60.7 jit_solution(5125379370771168021)
XLA Ops:
  0.6 0.0 copy-start.5
  0.6 3.2 %first.1 = bf16[8,9,8,128]{3,2,1,0:T(8,128)(2,1)} custom-call(s32[8,32]{1,0:T(8,128)} %bitcast.5, bf16[8,3200]{1,0:T(8,128)(2,1)} %refs_0_.1, f32[3,8]{1,0:T(4,128)} %refs_1_.2, s32[8,128]{1,0:T(8,128)} %bitcast.7, s32[8,128]{1,0:T(8,128)} %bitcast.8, f32[8,128]{1,0:T(8,128)} %bitcast.9, f32[8,128]{1,0:T(8,128)} %bitcast.10, bf16[2,640,640]{2,1,0:T(8,128)(2,1)} %refs_1_.3, ...), custom_call_target="tpu_custom_call" | custom-call | flops 50000000 | bytes 3000000 | tf_op jit(solution)/shard_map/first/pallas_call | solution.py:466
  3.8 11.2 %all_to_all.15.parts_ref.group_ref = bf16[8,9,8,128]{3,2,1,0:T(8,128)(2,1)S(1)} all-to-all(bf16[8,9,8,128]{3,2,1,0:T(8,128)(2,1)} %first.1), channel_id=1, replica_groups=mesh['y'=2,'zh'=4,'r'=4,'tgt'=8] {'y','r'}, dimensions={0} | all-to-all | bytes 294912 | tf_op jit(solution)/shard_map/all_to_all | solution.py:478
  15.0 0.9 %spread.1 = (bf16[8,30,8,128]{3,2,1,0:T(8,128)(2,1)}, bf16[8,128]{1,0:T(8,128)(2,1)S(1)}) custom-call(bf16[8,9,8,128]{3,2,1,0:T(8,128)(2,1)S(1)} %all_to_all.15.parts_ref.group_ref), custom_call_target="tpu_custom_call" | custom-call | bytes 800000 | tf_op jit(solution)/shard_map/spread/pallas_call | solution.py:481
  15.9 5.6 %all-to-all-start.1 = ((bf16[8,30,8,128]{3,2,1,0:T(8,128)(2,1)}), bf16[8,30,8,128]{3,2,1,0:T(8,128)(2,1)S(1)}, u32[]{:S(2)}, u32[]{:S(2)}) async-start(bf16[8,30,8,128]{3,2,1,0:T(8,128)(2,1)} %get-tuple-element.4), calls=%async_computation.1 | async-start | bytes 983040 | tf_op jit(solution)/shard_map/all_to_all | solution.py:490
  21.5 0.0 copy-start.6
  21.5 0.0 copy-start.7
  21.5 5.5 %collective-permute-start.2 = (bf16[8,128]{1,0:T(8,128)(2,1)S(1)}, bf16[8,128]{1,0:T(8,128)(2,1)S(1)}, u32[]{:S(2)}, u32[]{:S(2)}) collective-permute-start(bf16[8,128]{1,0:T(8,128)(2,1)S(1)} %get-tuple-element.5.pos_ref0), channel_id=1, source_target_pairs={{0,96},{32,0},{64,32},{96,64},{1,97},{33,1},{65,33},{97,65},{2,98}... | collective-permute-start | bytes 6152 | tf_op jit(solution)/shard_map/ppermute | solution.py:493
  27.0 1.0 %collective-permute-start.1 = (bf16[8,128]{1,0:T(8,128)(2,1)S(1)}, bf16[8,128]{1,0:T(8,128)(2,1)S(1)}, u32[]{:S(2)}, u32[]{:S(2)}) collective-permute-start(bf16[8,128]{1,0:T(8,128)(2,1)S(1)} %get-tuple-element.5.pos_ref0), channel_id=1, source_target_pairs={{0,64},{32,96},{64,0},{96,32},{1,65},{33,97},{65,1},{97,33},{2,66}... | collective-permute-start | bytes 6152 | tf_op jit(solution)/shard_map/ppermute | solution.py:493
  28.0 2.3 %collective-permute-start = (bf16[8,128]{1,0:T(8,128)(2,1)S(1)}, bf16[8,128]{1,0:T(8,128)(2,1)S(1)}, u32[]{:S(2)}, u32[]{:S(2)}) collective-permute-start(bf16[8,128]{1,0:T(8,128)(2,1)S(1)} %get-tuple-element.5.pos_ref0), channel_id=1, source_target_pairs={{0,32},{32,64},{64,96},{96,0},{1,33},{33,65},{65,97},{97,1},{2,34}... | collective-permute-start | bytes 6152 | tf_op jit(solution)/shard_map/ppermute | solution.py:493
  30.2 0.2 all-to-all-done.1.feats_ref
  30.5 0.0 copy-done.5
  30.5 4.1 %edge_sums.1.parts_ref = bf16[32,4,8,128]{3,2,1,0:T(8,128)(2,1)S(1)} custom-call(s32[8,32]{1,0:T(8,128)S(1)} %bitcast.6, bf16[8,30,8,128]{3,2,1,0:T(8,128)(2,1)S(1)} %all-to-all-done.1.feats_ref, bf16[8,9,8,128]{3,2,1,0:T(8,128)(2,1)S(1)} %all_to_all.15.parts_ref.group_ref), custom_call_target="tpu_custom_call" | custom-call | flops 8000000000 | bytes 2000000 | tf_op jit(solution)/shard_map/edge_sums/pallas_call | solution.py:496
  34.6 0.0 copy-start.2
  34.6 0.0 copy-start.3
  34.6 0.0 copy-start.4
  34.6 0.0 collective-permute-done.2.pos_ref3
  34.6 0.0 collective-permute-done.1.pos_ref2
  34.6 0.0 collective-permute-done.pos_ref1
  34.6 0.0 copy-done.6
  34.7 0.0 copy-done.7
  34.7 0.0 copy-start
  34.7 0.0 copy-start.1
  34.7 2.0 %message.1 = bf16[32,4,8,128]{3,2,1,0:T(8,128)(2,1)S(1)} custom-call(bf16[8,30,8,128]{3,2,1,0:T(8,128)(2,1)S(1)} %all-to-all-done.1.feats_ref, bf16[8,128]{1,0:T(8,128)(2,1)S(1)} %get-tuple-element.5.pos_ref0, bf16[8,128]{1,0:T(8,128)(2,1)S(1)} %collective-permute-done.pos_ref1, bf16[8,128]{1,0:T(8,128)(2,1)S(1)} %collective-permute-done.1.pos_ref2, ...), custom_call_target="tpu_custom_call" | custom-call | flops 3000000000 | bytes 1000000 | tf_op jit(solution)/shard_map/message/pallas_call | solution.py:517
  36.7 22.8 %all_to_all.16.refs_0_ = bf16[32,4,8,128]{3,2,1,0:T(8,128)(2,1)S(1)} all-to-all(bf16[32,4,8,128]{3,2,1,0:T(8,128)(2,1)S(1)} %message.1), channel_id=1, replica_groups=mesh['y'=2,'zh'=4,'r'=4,'tgt'=8] {'y','zh','r'}, dimensions={0} | all-to-all | bytes 524288 | tf_op jit(solution)/shard_map/all_to_all | solution.py:526
  59.5 0.0 copy-done.2
  59.5 0.0 copy-done.3
  59.5 0.0 copy-done.4
  59.5 0.0 copy-done
  59.5 0.0 copy-done.1
  59.5 1.2 %last_conv.1 = (bf16[8,3200]{1,0:T(8,128)(2,1)}, f32[8,128]{1,0:T(8,128)}) custom-call(bf16[32,4,8,128]{3,2,1,0:T(8,128)(2,1)S(1)} %all_to_all.16.refs_0_, bf16[2,640,640]{2,1,0:T(8,128)(2,1)S(1)} %copy-done.1, bf16[2,2,512,512]{3,2,1,0:T(8,128)(2,1)S(1)} %copy-done, bf16[2,2,384,384]{3,2,1,0:T(8,128)(2,1)S(1)} %copy-done.2, ...), custom_call_target="tpu_custom_call" | custom-call | flops 100000000 | bytes 3200000 | tf_op jit(solution)/shard_map/last_conv/pallas_call | solution.py:529
Async XLA Ops:
  0.6 29.8 %copy-start.5 = (s32[32,8]{0,1:T(8,128)S(1)}, s32[32,8]{0,1:T(8,128)}, u32[]{:S(2)}) copy-start(s32[32,8]{0,1:T(8,128)} %param.20) | copy-start | bytes 3076
  15.9 14.6 %all-to-all-start.1 = ((bf16[8,30,8,128]{3,2,1,0:T(8,128)(2,1)}), bf16[8,30,8,128]{3,2,1,0:T(8,128)(2,1)S(1)}, u32[]{:S(2)}, u32[]{:S(2)}) async-start(bf16[8,30,8,128]{3,2,1,0:T(8,128)(2,1)} %get-tuple-element.4), calls=%async_computation.1 | async-start | bytes 983040 | tf_op jit(solution)/shard_map/all_to_all | solution.py:490
  21.5 13.2 %copy-start.6 = (f32[2048,128]{1,0:T(8,128)S(1)}, f32[2048,128]{1,0:T(8,128)}, u32[]{:S(2)}) copy-start(f32[2048,128]{1,0:T(8,128)} %kfilter_ref.1) | copy-start | bytes 3145732
  21.5 13.2 %copy-start.7 = (s32[3,2048]{1,0:T(4,128)S(1)}, s32[3,2048]{1,0:T(4,128)}, u32[]{:S(2)}) copy-start(s32[3,2048]{1,0:T(4,128)} %kidx_ref.1) | copy-start | bytes 73732
  21.5 13.1 %collective-permute-start.2 = (bf16[8,128]{1,0:T(8,128)(2,1)S(1)}, bf16[8,128]{1,0:T(8,128)(2,1)S(1)}, u32[]{:S(2)}, u32[]{:S(2)}) collective-permute-start(bf16[8,128]{1,0:T(8,128)(2,1)S(1)} %get-tuple-element.5.pos_ref0), channel_id=1, source_target_pairs={{0,96},{32,0},{64,32},{96,64},{1,97},{33,1},{65,33},{97,65},{2,98}... | collective-permute-start | bytes 6152 | tf_op jit(solution)/shard_map/ppermute | solution.py:493
  27.0 7.7 %collective-permute-start.1 = (bf16[8,128]{1,0:T(8,128)(2,1)S(1)}, bf16[8,128]{1,0:T(8,128)(2,1)S(1)}, u32[]{:S(2)}, u32[]{:S(2)}) collective-permute-start(bf16[8,128]{1,0:T(8,128)(2,1)S(1)} %get-tuple-element.5.pos_ref0), channel_id=1, source_target_pairs={{0,64},{32,96},{64,0},{96,32},{1,65},{33,97},{65,1},{97,33},{2,66}... | collective-permute-start | bytes 6152 | tf_op jit(solution)/shard_map/ppermute | solution.py:493
  28.0 6.7 %collective-permute-start = (bf16[8,128]{1,0:T(8,128)(2,1)S(1)}, bf16[8,128]{1,0:T(8,128)(2,1)S(1)}, u32[]{:S(2)}, u32[]{:S(2)}) collective-permute-start(bf16[8,128]{1,0:T(8,128)(2,1)S(1)} %get-tuple-element.5.pos_ref0), channel_id=1, source_target_pairs={{0,32},{32,64},{64,96},{96,0},{1,33},{33,65},{65,97},{97,1},{2,34}... | collective-permute-start | bytes 6152 | tf_op jit(solution)/shard_map/ppermute | solution.py:493
  34.6 24.9 %copy-start.2 = (bf16[2,2,384,384]{3,2,1,0:T(8,128)(2,1)S(1)}, bf16[2,2,384,384]{3,2,1,0:T(8,128)(2,1)}, u32[]{:S(2)}) copy-start(bf16[2,2,384,384]{3,2,1,0:T(8,128)(2,1)} %refs_3_.1) | copy-start | bytes 3538948
  34.6 24.9 %copy-start.3 = (bf16[2,2,256,256]{3,2,1,0:T(8,128)(2,1)S(1)}, bf16[2,2,256,256]{3,2,1,0:T(8,128)(2,1)}, u32[]{:S(2)}) copy-start(bf16[2,2,256,256]{3,2,1,0:T(8,128)(2,1)} %refs_4_.1) | copy-start | bytes 1572868
  34.6 24.9 %copy-start.4 = (bf16[2,2,128,128]{3,2,1,0:T(8,128)(2,1)S(1)}, bf16[2,2,128,128]{3,2,1,0:T(8,128)(2,1)}, u32[]{:S(2)}) copy-start(bf16[2,2,128,128]{3,2,1,0:T(8,128)(2,1)} %refs_5_.1) | copy-start | bytes 393220
  34.7 24.8 %copy-start = (bf16[2,2,512,512]{3,2,1,0:T(8,128)(2,1)S(1)}, bf16[2,2,512,512]{3,2,1,0:T(8,128)(2,1)}, u32[]{:S(2)}) copy-start(bf16[2,2,512,512]{3,2,1,0:T(8,128)(2,1)} %refs_2_.1) | copy-start | bytes 6291460
  34.7 24.8 %copy-start.1 = (bf16[2,640,640]{2,1,0:T(8,128)(2,1)S(1)}, bf16[2,640,640]{2,1,0:T(8,128)(2,1)}, u32[]{:S(2)}) copy-start(bf16[2,640,640]{2,1,0:T(8,128)(2,1)} %refs_1_.3) | copy-start | bytes 4915204

commit v5 on v4

--- a/solution.py
+++ b/solution.py
@@ -67,11 +67,6 @@
     return 1.0 - s * s, s * series(COS_TERMS, x2)
 
 
-def split2(value):
-    high = value.astype(BF16)
-    return high, (value - high.astype(F32)).astype(BF16)
-
-
 def position_tile(pos_ref):
     row_ids = lax.broadcasted_iota(jnp.int32, (ROWS, ROWS), 0)
     col_ids = lax.broadcasted_iota(jnp.int32, (ROWS, ROWS), 1)
@@ -379,15 +374,14 @@
         even = jnp.dot(table[:, :atoms], charges, preferred_element_type=F32)
         odd = jnp.dot(table[:, atoms:], charges, preferred_element_type=F32)
         own_table = own_table.astype(BF16)
-        for part in split2(filters * (even + pltpu.roll(odd, HALF_ROW, 1))):
-            total = total + jnp.dot(own_table, part, preferred_element_type=F32)
+        factors = (filters * (even + pltpu.roll(odd, HALF_ROW, 1))).astype(BF16)
+        total = total + jnp.dot(own_table, factors, preferred_element_type=F32)
     total = in_mix(pltpu.roll(total, MIX_LANE, 1))
     for shift in range(ZH):
         from_zone = (zone + ZH - shift) % ZH
         for y in range(Y):
             low = (shift * SLICES + y * R) * ROWS
             place = pl.ds(y * ZH * R + from_zone * R, R)
-            out_ref[place, :3, :, :] = parts_ref[place, :3, :, :]
             out_ref[place, 3, :, :] = (
                 parts_ref[place, 3, :, :].astype(F32) + total[low : low + R * ROWS].reshape(R, ROWS, LANES)
             ).astype(BF16)
@@ -521,6 +515,7 @@
         out_specs=vmem,
         compiler_params=params(32),
         cost_estimate=COST["message"],
+        input_output_aliases={7: 0},
         name="message",
     )(feats, *zones, k_index, k_filter, parts)
     parts = lax.all_to_all(parts, SRC_AXES, 0, 0)

time: 61 us -> 60.9 us (level)
  no operation moved by 1% of the time
where the time goes in v5:
time: 60.9 us; the launch traced here: 60.5 us
  blocking collectives  34 us (56%)
  starting transfers between devices  14.3 us (23%)
  Pallas kernels  11.2 us (18%)
  between operations  0.78 us (1%)
    all_to_all x1, blocking collectives, body(): parts = lax.all_to_all(parts, SRC_AXES, 0, 0)  22.8 us
    all_to_all x1, blocking collectives, body(): group = lax.all_to_all(group, ('y', 'r'), 0, 0)  11.2 us
    ppermute x3, starting transfers between devices, body(): lax.ppermute(pos, 'zh', [(i, (i + shift) % ZH) for i in range(ZH)])  8.73 us
    all_to_all x1, starting transfers between devices, body(): feats = lax.all_to_all(feats, 'tgt', 0, 0)  5.56 us
    pallas_call x1, Pallas kernels, body(): pl.pallas_call(main_kernel, out_shape=jax.ShapeDtypeStruct(parts_out, BF1...  4.11 us
    pallas_call x1, Pallas kernels, body(): pl.pallas_call(first_kernel, out_shape=jax.ShapeDtypeStruct(group_out, BF...  3.18 us
    pallas_call x1, Pallas kernels, body(): pl.pallas_call(message_kernel, out_shape=jax.ShapeDtypeStruct(parts_out,...  1.83 us
  transfers between devices with their start and end apart: 4, of which 1 were waited for; matrix products, arithmetic and copies ran while one was open for 0% of the time, Pallas kernels for 7%

profile of v5, /device:TPU:1, one launch (start us, length us, event | category | flops | bytes accessed | tf_op | source)
XLA Modules:
  0.0 60.5 jit_solution(15419535420775110251)
XLA Ops:
  0.6 0.0 copy-start.5
  0.6 3.2 %first.1 = bf16[8,9,8,128]{3,2,1,0:T(8,128)(2,1)} custom-call(s32[8,32]{1,0:T(8,128)} %bitcast.5, bf16[8,3200]{1,0:T(8,128)(2,1)} %refs_0_.1, f32[3,8]{1,0:T(4,128)} %refs_1_.2, s32[8,128]{1,0:T(8,128)} %bitcast.7, s32[8,128]{1,0:T(8,128)} %bitcast.8, f32[8,128]{1,0:T(8,128)} %bitcast.9, f32[8,128]{1,0:T(8,128)} %bitcast.10, bf16[2,640,640]{2,1,0:T(8,128)(2,1)} %refs_1_.3, ...), custom_call_target="tpu_custom_call" | custom-call | flops 50000000 | bytes 3000000 | tf_op jit(solution)/shard_map/first/pallas_call | solution.py:460
  3.8 11.2 %all_to_all.15.parts_ref.group_ref = bf16[8,9,8,128]{3,2,1,0:T(8,128)(2,1)S(1)} all-to-all(bf16[8,9,8,128]{3,2,1,0:T(8,128)(2,1)} %first.1), channel_id=1, replica_groups=mesh['y'=2,'zh'=4,'r'=4,'tgt'=8] {'y','r'}, dimensions={0} | all-to-all | bytes 294912 | tf_op jit(solution)/shard_map/all_to_all | solution.py:472
  15.0 0.9 %spread.1 = (bf16[8,30,8,128]{3,2,1,0:T(8,128)(2,1)}, bf16[8,128]{1,0:T(8,128)(2,1)S(1)}) custom-call(bf16[8,9,8,128]{3,2,1,0:T(8,128)(2,1)S(1)} %all_to_all.15.parts_ref.group_ref), custom_call_target="tpu_custom_call" | custom-call | bytes 800000 | tf_op jit(solution)/shard_map/spread/pallas_call | solution.py:475
  15.9 5.6 %all-to-all-start.1 = ((bf16[8,30,8,128]{3,2,1,0:T(8,128)(2,1)}), bf16[8,30,8,128]{3,2,1,0:T(8,128)(2,1)S(1)}, u32[]{:S(2)}, u32[]{:S(2)}) async-start(bf16[8,30,8,128]{3,2,1,0:T(8,128)(2,1)} %get-tuple-element.4), calls=%async_computation.1 | async-start | bytes 983040 | tf_op jit(solution)/shard_map/all_to_all | solution.py:484
  21.5 0.0 copy-start.6
  21.5 0.0 copy-start.7
  21.5 5.5 %collective-permute-start.2 = (bf16[8,128]{1,0:T(8,128)(2,1)S(1)}, bf16[8,128]{1,0:T(8,128)(2,1)S(1)}, u32[]{:S(2)}, u32[]{:S(2)}) collective-permute-start(bf16[8,128]{1,0:T(8,128)(2,1)S(1)} %get-tuple-element.5.pos_ref0), channel_id=1, source_target_pairs={{0,96},{32,0},{64,32},{96,64},{1,97},{33,1},{65,33},{97,65},{2,98}... | collective-permute-start | bytes 6152 | tf_op jit(solution)/shard_map/ppermute | solution.py:487
  27.0 1.0 %collective-permute-start.1 = (bf16[8,128]{1,0:T(8,128)(2,1)S(1)}, bf16[8,128]{1,0:T(8,128)(2,1)S(1)}, u32[]{:S(2)}, u32[]{:S(2)}) collective-permute-start(bf16[8,128]{1,0:T(8,128)(2,1)S(1)} %get-tuple-element.5.pos_ref0), channel_id=1, source_target_pairs={{0,64},{32,96},{64,0},{96,32},{1,65},{33,97},{65,1},{97,33},{2,66}... | collective-permute-start | bytes 6152 | tf_op jit(solution)/shard_map/ppermute | solution.py:487
  28.0 2.3 %collective-permute-start = (bf16[8,128]{1,0:T(8,128)(2,1)S(1)}, bf16[8,128]{1,0:T(8,128)(2,1)S(1)}, u32[]{:S(2)}, u32[]{:S(2)}) collective-permute-start(bf16[8,128]{1,0:T(8,128)(2,1)S(1)} %get-tuple-element.5.pos_ref0), channel_id=1, source_target_pairs={{0,32},{32,64},{64,96},{96,0},{1,33},{33,65},{65,97},{97,1},{2,34}... | collective-permute-start | bytes 6152 | tf_op jit(solution)/shard_map/ppermute | solution.py:487
  30.2 0.2 all-to-all-done.1.feats_ref
  30.5 0.0 copy-done.5
  30.5 4.1 %edge_sums.1.parts_ref = bf16[32,4,8,128]{3,2,1,0:T(8,128)(2,1)S(1)} custom-call(s32[8,32]{1,0:T(8,128)S(1)} %bitcast.6, bf16[8,30,8,128]{3,2,1,0:T(8,128)(2,1)S(1)} %all-to-all-done.1.feats_ref, bf16[8,9,8,128]{3,2,1,0:T(8,128)(2,1)S(1)} %all_to_all.15.parts_ref.group_ref), custom_call_target="tpu_custom_call" | custom-call | flops 8000000000 | bytes 2000000 | tf_op jit(solution)/shard_map/edge_sums/pallas_call | solution.py:490
  34.6 0.0 copy-start.2
  34.6 0.0 copy-start.3
  34.6 0.0 copy-start.4
  34.6 0.0 collective-permute-done.2.pos_ref3
  34.6 0.0 collective-permute-done.1.pos_ref2
  34.6 0.0 collective-permute-done.pos_ref1
  34.6 0.0 copy-done.6
  34.7 0.0 copy-done.7
  34.7 0.0 copy-start
  34.7 0.0 copy-start.1
  34.7 1.8 %message.1 = bf16[32,4,8,128]{3,2,1,0:T(8,128)(2,1)S(1)} custom-call(bf16[8,30,8,128]{3,2,1,0:T(8,128)(2,1)S(1)} %all-to-all-done.1.feats_ref, bf16[8,128]{1,0:T(8,128)(2,1)S(1)} %get-tuple-element.5.pos_ref0, bf16[8,128]{1,0:T(8,128)(2,1)S(1)} %collective-permute-done.pos_ref1, ...), custom_call_target="tpu_custom_call", output_to_operand_aliasing={{}: (7, {})} | custom-call | flops 3000000000 | bytes 1000000 | tf_op jit(solution)/shard_map/message/pallas_call | solution.py:511
  36.5 22.8 %all_to_all.16.refs_0_ = bf16[32,4,8,128]{3,2,1,0:T(8,128)(2,1)S(1)} all-to-all(bf16[32,4,8,128]{3,2,1,0:T(8,128)(2,1)S(1)} %message.1), channel_id=1, replica_groups=mesh['y'=2,'zh'=4,'r'=4,'tgt'=8] {'y','zh','r'}, dimensions={0} | all-to-all | bytes 524288 | tf_op jit(solution)/shard_map/all_to_all | solution.py:521
  59.3 0.0 copy-done.2
  59.3 0.0 copy-done.3
  59.3 0.0 copy-done.4
  59.3 0.0 copy-done
  59.3 0.0 copy-done.1
  59.3 1.2 %last_conv.1 = (bf16[8,3200]{1,0:T(8,128)(2,1)}, f32[8,128]{1,0:T(8,128)}) custom-call(bf16[32,4,8,128]{3,2,1,0:T(8,128)(2,1)S(1)} %all_to_all.16.refs_0_, bf16[2,640,640]{2,1,0:T(8,128)(2,1)S(1)} %copy-done.1, bf16[2,2,512,512]{3,2,1,0:T(8,128)(2,1)S(1)} %copy-done, bf16[2,2,384,384]{3,2,1,0:T(8,128)(2,1)S(1)} %copy-done.2, ...), custom_call_target="tpu_custom_call" | custom-call | flops 100000000 | bytes 3200000 | tf_op jit(solution)/shard_map/last_conv/pallas_call | solution.py:524
Async XLA Ops:
  0.6 29.8 %copy-start.5 = (s32[32,8]{0,1:T(8,128)S(1)}, s32[32,8]{0,1:T(8,128)}, u32[]{:S(2)}) copy-start(s32[32,8]{0,1:T(8,128)} %param.20) | copy-start | bytes 3076
  15.9 14.6 %all-to-all-start.1 = ((bf16[8,30,8,128]{3,2,1,0:T(8,128)(2,1)}), bf16[8,30,8,128]{3,2,1,0:T(8,128)(2,1)S(1)}, u32[]{:S(2)}, u32[]{:S(2)}) async-start(bf16[8,30,8,128]{3,2,1,0:T(8,128)(2,1)} %get-tuple-element.4), calls=%async_computation.1 | async-start | bytes 983040 | tf_op jit(solution)/shard_map/all_to_all | solution.py:484
  21.5 13.2 %copy-start.6 = (f32[2048,128]{1,0:T(8,128)S(1)}, f32[2048,128]{1,0:T(8,128)}, u32[]{:S(2)}) copy-start(f32[2048,128]{1,0:T(8,128)} %kfilter_ref.1) | copy-start | bytes 3145732
  21.5 13.2 %copy-start.7 = (s32[3,2048]{1,0:T(4,128)S(1)}, s32[3,2048]{1,0:T(4,128)}, u32[]{:S(2)}) copy-start(s32[3,2048]{1,0:T(4,128)} %kidx_ref.1) | copy-start | bytes 73732
  21.5 13.1 %collective-permute-start.2 = (bf16[8,128]{1,0:T(8,128)(2,1)S(1)}, bf16[8,128]{1,0:T(8,128)(2,1)S(1)}, u32[]{:S(2)}, u32[]{:S(2)}) collective-permute-start(bf16[8,128]{1,0:T(8,128)(2,1)S(1)} %get-tuple-element.5.pos_ref0), channel_id=1, source_target_pairs={{0,96},{32,0},{64,32},{96,64},{1,97},{33,1},{65,33},{97,65},{2,98}... | collective-permute-start | bytes 6152 | tf_op jit(solution)/shard_map/ppermute | solution.py:487
  27.0 7.7 %collective-permute-start.1 = (bf16[8,128]{1,0:T(8,128)(2,1)S(1)}, bf16[8,128]{1,0:T(8,128)(2,1)S(1)}, u32[]{:S(2)}, u32[]{:S(2)}) collective-permute-start(bf16[8,128]{1,0:T(8,128)(2,1)S(1)} %get-tuple-element.5.pos_ref0), channel_id=1, source_target_pairs={{0,64},{32,96},{64,0},{96,32},{1,65},{33,97},{65,1},{97,33},{2,66}... | collective-permute-start | bytes 6152 | tf_op jit(solution)/shard_map/ppermute | solution.py:487
  28.0 6.7 %collective-permute-start = (bf16[8,128]{1,0:T(8,128)(2,1)S(1)}, bf16[8,128]{1,0:T(8,128)(2,1)S(1)}, u32[]{:S(2)}, u32[]{:S(2)}) collective-permute-start(bf16[8,128]{1,0:T(8,128)(2,1)S(1)} %get-tuple-element.5.pos_ref0), channel_id=1, source_target_pairs={{0,32},{32,64},{64,96},{96,0},{1,33},{33,65},{65,97},{97,1},{2,34}... | collective-permute-start | bytes 6152 | tf_op jit(solution)/shard_map/ppermute | solution.py:487
  34.6 24.7 %copy-start.2 = (bf16[2,2,384,384]{3,2,1,0:T(8,128)(2,1)S(1)}, bf16[2,2,384,384]{3,2,1,0:T(8,128)(2,1)}, u32[]{:S(2)}) copy-start(bf16[2,2,384,384]{3,2,1,0:T(8,128)(2,1)} %refs_3_.1) | copy-start | bytes 3538948
  34.6 24.7 %copy-start.3 = (bf16[2,2,256,256]{3,2,1,0:T(8,128)(2,1)S(1)}, bf16[2,2,256,256]{3,2,1,0:T(8,128)(2,1)}, u32[]{:S(2)}) copy-start(bf16[2,2,256,256]{3,2,1,0:T(8,128)(2,1)} %refs_4_.1) | copy-start | bytes 1572868
  34.6 24.7 %copy-start.4 = (bf16[2,2,128,128]{3,2,1,0:T(8,128)(2,1)S(1)}, bf16[2,2,128,128]{3,2,1,0:T(8,128)(2,1)}, u32[]{:S(2)}) copy-start(bf16[2,2,128,128]{3,2,1,0:T(8,128)(2,1)} %refs_5_.1) | copy-start | bytes 393220
  34.7 24.7 %copy-start = (bf16[2,2,512,512]{3,2,1,0:T(8,128)(2,1)S(1)}, bf16[2,2,512,512]{3,2,1,0:T(8,128)(2,1)}, u32[]{:S(2)}) copy-start(bf16[2,2,512,512]{3,2,1,0:T(8,128)(2,1)} %refs_2_.1) | copy-start | bytes 6291460
  34.7 24.7 %copy-start.1 = (bf16[2,640,640]{2,1,0:T(8,128)(2,1)S(1)}, bf16[2,640,640]{2,1,0:T(8,128)(2,1)}, u32[]{:S(2)}) copy-start(bf16[2,640,640]{2,1,0:T(8,128)(2,1)} %refs_1_.3) | copy-start | bytes 4915204
